TPU v7x, 8 devices: a whole 2x2x1 slice. The times are simulated.
8 devices in a mesh: pod: 1 (over z), data: 2 (over y), model: 4 (over x, core).
Axes of the slice: x: 2, y: 2, z: 1, core: 2. Of those that a mesh axis runs over, the one named last changes fastest.
Arguments:
- x_in: bfloat16 [2, 1024, 2048], P(('pod', 'data'), 'model')
- dy_in: bfloat16 [2, 1024, 2048], P(('pod', 'data'), 'model')
- w_q: bfloat16 [2048, 8, 256], P(None, 'model')
- w_k: bfloat16 [1, 2048, 256], replicated
- w_v: bfloat16 [1, 2048, 256], replicated
- w_o: bfloat16 [8, 256, 2048], P('model')
Outputs:
- output 1: bfloat16 [2, 1024, 2048], P(('pod', 'data'), 'model')
- output 2: float32 [2048, 8, 256], P(('pod', 'data'), 'model')
- output 3: float32 [2048, 256], P(('pod', 'model', 'data'))
- output 4: float32 [2048, 256], P(('pod', 'model', 'data'))
- output 5: float32 [8, 256, 2048], P(('pod', 'model'), None, 'data')
All inputs are finite; a program needn't handle non-finite values.
Results may differ from a plain program's by a relative error of at most 0.00941715.
Values are sent between devices in bfloat16 or wider.
A program may use at most 1 GiB of HBM per device.

v0:
```python
import jax
import jax.numpy as jnp
from jax import lax
from jax.sharding import PartitionSpec as P


def subgroup_pairs(step_shift, sub_size, axis_size):
    return [(start_dev + member, start_dev + (member + step_shift) % sub_size)
            for start_dev in range(0, axis_size, sub_size) for member in range(sub_size)]


def subgroup_scatter_sum(grad_parts, sub_size, axis_size):
    my_slot = lax.axis_index('model') % sub_size
    lead_dim, row_count, col_count = grad_parts.shape
    row_blocks = grad_parts.reshape(lead_dim, sub_size, row_count // sub_size, col_count)
    total_sum = lax.dynamic_index_in_dim(row_blocks, my_slot, axis=1, keepdims=False)
    for step_shift in range(1, sub_size):
        outgoing = lax.dynamic_index_in_dim(row_blocks, (my_slot + step_shift) % sub_size, axis=1, keepdims=False)
        total_sum = total_sum + lax.ppermute(outgoing, 'model', subgroup_pairs(step_shift, sub_size, axis_size))
    return total_sum


def solution(mesh):
    model_size = mesh.shape['model']
    tok_spec = P(('pod', 'data'), 'model', None)

    def device_step(x_loc, dy_loc, w_q, w_k, w_v, w_o):
        kv_heads = w_k.shape[0]
        head_dim = w_k.shape[2]
        sub_size = model_size // kv_heads
        score_scale = head_dim ** -0.5
        kv_index = lax.axis_index('model') // sub_size
        x_full = lax.all_gather(x_loc, 'model', axis=1, tiled=True)
        dy_full = lax.all_gather(dy_loc, 'model', axis=1, tiled=True)
        kv_weights = jnp.stack([lax.dynamic_index_in_dim(w_k, kv_index, axis=0, keepdims=False),
                                lax.dynamic_index_in_dim(w_v, kv_index, axis=0, keepdims=False)])
        seq_len = x_full.shape[1]
        causal = lax.broadcasted_iota(jnp.int32, (seq_len, seq_len), 0) >= lax.broadcasted_iota(jnp.int32, (seq_len, seq_len), 1)
        q_loc = jnp.einsum('btd,dhe->bhte', x_full, w_q, preferred_element_type=jnp.float32).astype(jnp.bfloat16)
        kv_loc = jnp.einsum('btd,nde->nbte', x_full, kv_weights, preferred_element_type=jnp.float32).astype(jnp.bfloat16)
        k_loc = kv_loc[0]
        v_loc = kv_loc[1]
        scores = jnp.einsum('bhqe,bke->bhqk', q_loc, k_loc, preferred_element_type=jnp.float32) * score_scale
        attn_prob = jax.nn.softmax(jnp.where(causal, scores, -jnp.inf), axis=-1)
        prob_bf = attn_prob.astype(jnp.bfloat16)
        out_loc = jnp.einsum('bhqk,bke->bhqe', prob_bf, v_loc, preferred_element_type=jnp.float32).astype(jnp.bfloat16)
        dout_loc = jnp.einsum('btd,hed->bhte', dy_full, w_o, preferred_element_type=jnp.float32).astype(jnp.bfloat16)
        grad_prob = jnp.einsum('bhqe,bke->bhqk', dout_loc, v_loc, preferred_element_type=jnp.float32)
        row_delta = jnp.einsum('bhqe,bhqe->bhq', dout_loc, out_loc, preferred_element_type=jnp.float32)
        grad_score = (attn_prob * (grad_prob - row_delta[..., None])).astype(jnp.bfloat16)
        grad_q = (jnp.einsum('bhqk,bke->bhqe', grad_score, k_loc, preferred_element_type=jnp.float32) * score_scale).astype(jnp.bfloat16)
        grad_k = jnp.einsum('bhqk,bhqe->bke', grad_score, q_loc, preferred_element_type=jnp.float32) * score_scale
        grad_v = jnp.einsum('bhqk,bhqe->bke', prob_bf, dout_loc, preferred_element_type=jnp.float32)
        grad_kv = jnp.stack([grad_k, grad_v]).astype(jnp.bfloat16)
        dx_part = (jnp.einsum('bhte,dhe->btd', grad_q, w_q, preferred_element_type=jnp.float32)
                   + jnp.einsum('nbte,nde->btd', grad_kv, kv_weights, preferred_element_type=jnp.float32))
        dwq_part = jnp.einsum('btd,bhte->dhe', x_full, grad_q, preferred_element_type=jnp.float32)
        dwkv_part = jnp.einsum('btd,nbte->nde', x_full, grad_kv, preferred_element_type=jnp.float32)
        dwo_part = jnp.einsum('bhte,btd->hed', out_loc, dy_full, preferred_element_type=jnp.float32)
        dx_loc = lax.psum_scatter(dx_part, 'model', scatter_dimension=1, tiled=True).astype(jnp.bfloat16)
        dwkv_sub = subgroup_scatter_sum(dwkv_part, sub_size, model_size)
        dwkv_loc = lax.psum_scatter(dwkv_sub, 'data', scatter_dimension=1, tiled=True)
        dwq_loc = lax.psum_scatter(dwq_part, 'data', scatter_dimension=0, tiled=True)
        dwo_loc = lax.psum_scatter(dwo_part, 'data', scatter_dimension=2, tiled=True)
        return dx_loc, dwq_loc, dwkv_loc[0], dwkv_loc[1], dwo_loc

    kv_rows = P(('pod', 'model', 'data'), None)
    return jax.shard_map(device_step, mesh=mesh,
                         in_specs=(tok_spec, tok_spec, P(None, 'model', None), P(), P(), P('model', None, None)),
                         out_specs=(tok_spec, P(('pod', 'data'), 'model', None), kv_rows, kv_rows, P(('pod', 'model'), None, 'data')),
                         check_vma=False)
```

profile of v0, /device:TPU:0, one launch (start us, length us, event | category | flops | bytes accessed | tf_op | source)
XLA Modules:
  0.0 388.7 jit_solution(3337064300865696419)
XLA Ops:
  7.2 0.0 copy-start
  7.2 0.0 all-gather.5.cloned.1.call-start
  7.2 0.7 all-gather.5.cloned.1.call-update
  7.9 0.0 all-gather.3.cloned.1.call-start
  8.0 0.7 all-gather.3.cloned.1.call-update
  8.7 0.0 reduce-scatter.9.cloned.1.call-start
  8.8 1.5 copy.12
  10.3 2.7 copy.13
  12.9 1.3 iota_compare_fusion
  14.2 29.7 %all-gather.5.cloned.1.call-done = bf16[1,1024,2048]{2,1,0:T(8,128)(2,1)} async-done(((bf16[1,256,2048]{2,1,0:T(8,128)(2,1)}), bf16[1,1024,2048]{2,1,0:T(8,128)(2,1)}) %all-gather.5.cloned.1.call-update) | async-done | bytes 4194320 | tf_op jit(solution)/shard_map/all_gather | solution.py:34
  43.9 5.5 %fusion.39 = bf16[2,1024,256]{1,2,0:T(8,128)(2,1)} fusion(bf16[2,256,2048]{2,1,0:T(8,128)(2,1)S(1)} %copy-done, bf16[1,1024,2048]{2,1,0:T(8,128)(2,1)} %all-gather.5.cloned.1.call-done), kind=kOutput, calls=%fused_computation.37 | convolution fusion | flops 2148007936 | bytes 7340032 | tf_op jit(solution)/shard_map/btd,hed->bhte/dot_general | solution.py:47
  49.4 2.6 copy.45
  52.0 25.0 %all-gather.3.cloned.1.call-done = bf16[1,1024,2048]{2,1,0:T(8,128)(2,1)} async-done(((bf16[1,256,2048]{2,1,0:T(8,128)(2,1)}), bf16[1,1024,2048]{2,1,0:T(8,128)(2,1)}) %all-gather.3.cloned.1.call-update) | async-done | bytes 4194320 | tf_op jit(solution)/shard_map/all_gather | solution.py:33
  76.9 6.3 %fusion.45 = bf16[2,1024,256]{1,2,0:T(8,128)(2,1)} fusion(bf16[1,1024,2048]{2,1,0:T(8,128)(2,1)} %all-gather.3.cloned.1.call-done, bf16[2048,2,256]{2,1,0:T(2,128)(2,1)} %param.8), kind=kOutput, calls=%fused_computation.39 | convolution fusion | flops 2148007936 | bytes 7340032 | tf_op jit(solution)/shard_map/btd,dhe->bhte/dot_general | solution.py:39
  83.3 0.0 copy-start.17
  83.3 3.5 fusion.42
  86.8 7.4 %fusion.65 = (f32[2,1024]{1,0:T(2,128)S(1)}, f32[2,1024,1024]{1,2,0:T(8,128)}) fusion(pred[1024,1024]{0,1:T(8,128)(4,1)S(1)} %copy-done.17, bf16[2,1024,256]{1,2,0:T(8,128)(2,1)} %fusion.45, bf16[2,1,1024,256]{2,3,0,1:T(8,128)(2,1)} %fusion.42), kind=kOutput, calls=%fused_computation.66 | convolution fusion | flops 1082131456 | bytes 11018240 | tf_op jit(solution)/shard_map/sub | solution.py:44
  94.2 4.8 %fusion.18 = bf16[2,1024,1024]{1,2,0:T(8,128)(2,1)S(1)} fusion(f32[2,1024,1024]{1,2,0:T(8,128)} %get-tuple-element.17, f32[2,1024]{1,0:T(2,128)S(1)} %get-tuple-element.16), kind=kLoop, calls=%fused_computation.24 | loop fusion | flops 4194304 | bytes 12591104 | tf_op jit(solution)/shard_map/convert_element_type | solution.py:45
  99.1 0.0 copy-start.13
  99.1 0.0 slice-start.1
  99.1 1.3 fusion.53
  100.4 0.3 copy-done.13
  100.7 0.3 copy-done.18
  100.9 2.5 multiply_reduce_fusion
  103.4 1.7 multiply_convert_fusion
  105.2 1.3 fusion.54
  106.5 0.8 copy-done.19
  107.3 1.6 copy-done.3
  108.9 4.5 %fusion.22 = f32[2,2048,256]{1,2,0:T(8,128)} fusion(bf16[1,1024,2048]{2,1,0:T(8,128)(2,1)S(1)} %copy-done.3, bf16[1,1024,256]{2,1,0:T(8,128)(2,1)S(1)} %fusion.53, bf16[1,1024,256]{2,1,0:T(8,128)(2,1)S(1)} %fusion.54), kind=kOutput, calls=%fused_computation.26 | convolution fusion | flops 2148007936 | bytes 9437184 | tf_op jit(solution)/shard_map/btd,nbte->nde/dot_general | solution.py:58
  113.4 6.0 %reshape.132 = f32[2,4,512,256]{2,1,3,0:T(4,128)} reshape(f32[2,2048,256]{1,2,0:T(8,128)} %fusion.22) | data formatting | bytes 8388608 | tf_op jit(solution)/shard_map/reshape | solution.py:15
  119.4 11.4 %constant_dynamic-slice_fusion.3 = (f32[2,1,512,256]{2,1,3,0:T(1,128)S(1)}, f32[2,1,512,256]{2,1,3,0:T(1,128)}, f32[2,1,512,256]{2,1,3,0:T(1,128)S(1)}, f32[2,1,512,256]{2,1,3,0:T(1,128)S(1)}) fusion(f32[2,4,512,256]{2,1,3,0:T(4,128)} %reshape.132, s32[]{:T(128)S(6)} %select_n.44, s32[]{:T(128)S(6)} %select_n.50, s32[]{:T(128)S(6)} %select_n.48, s32[]{:T(128)S(6)} %select_n.46), kind=kLoop, calls=%fused_computation.60 | loop fusion | bytes 8388624 | tf_op jit(solution)/shard_map/jit(dynamic_index_in_dim)/dynamic_slice | solution.py:16
  130.7 3.6 copy.32
  134.3 2.1 copy.31
  136.4 2.1 copy.30
  138.5 0.2 collective-permute-start
  138.8 0.4 collective-permute-start.1
  139.2 1.2 collective-permute-start.2
  140.4 0.9 copy.29
  141.3 21.9 %collective-permute-done = f32[2,512,256]{2,1,0:T(8,128)S(1)} collective-permute-done((f32[2,512,256]{2,1,0:T(8,128)}, f32[2,512,256]{2,1,0:T(8,128)S(1)}, u32[]{:S(2)}, u32[]{:S(2)}) %collective-permute-start) | collective-permute-done | bytes 1048608 | tf_op jit(solution)/shard_map/ppermute | solution.py:19
  163.2 1.6 collective-permute-done.1
  164.8 19.5 %collective-permute-done.2 = f32[2,512,256]{2,1,0:T(8,128)} collective-permute-done((f32[2,512,256]{2,1,0:T(8,128)}, f32[2,512,256]{2,1,0:T(8,128)}, u32[]{:S(2)}, u32[]{:S(2)}) %collective-permute-start.2) | collective-permute-done | bytes 1048608 | tf_op jit(solution)/shard_map/ppermute | solution.py:19
  184.3 2.8 fusion.56
  187.1 0.0 reduce-scatter.9.cloned.1.call-update
  187.2 0.3 reduce-scatter.7.cloned.1.call-start
  187.5 3.8 multiply_convert_fusion.1
  191.3 0.0 copy-start.15
  191.3 4.4 %fusion.19 = f32[2048,2,256]{0,2,1:T(8,128)} fusion(bf16[2,1024,256]{2,1,0:T(8,128)(2,1)S(1)} %multiply_convert_fusion.1, bf16[1,1024,2048]{2,1,0:T(8,128)(2,1)S(1)} %copy-done.4), kind=kOutput, calls=%fused_computation.25 | convolution fusion | flops 2147483648 | bytes 9437184 | tf_op jit(solution)/shard_map/btd,bhte->dhe/dot_general | solution.py:57
  195.7 0.0 reduce-scatter.7.cloned.1.call-update
  195.7 0.0 reduce-scatter.5.cloned.1.call-start
  195.8 4.4 %fusion.26 = f32[1024,2048,1]{1,0,2:T(8,128)S(1)} fusion(bf16[2,1024,256]{2,1,0:T(8,128)(2,1)} %copy-done.15, bf16[2048,2,256]{2,1,0:T(2,128)(2,1)} %param.8), kind=kOutput, calls=%fused_computation.31 | convolution fusion | flops 2147483648 | bytes 11534336 | tf_op jit(solution)/shard_map/bhte,dhe->btd/dot_general | solution.py:55
  200.3 5.7 %fusion.1 = f32[1,1024,2048]{2,1,0:T(8,128)} fusion(f32[1024,2048,1]{1,0,2:T(8,128)S(1)} %fusion.26, bf16[1,2048,256]{1,2,0:T(8,128)(2,1)S(1)} %copy-done.8, bf16[1,2048,256]{1,2,0:T(8,128)(2,1)S(1)} %copy-done.6, bf16[1,1024,256]{2,1,0:T(8,128)(2,1)S(1)} %copy-done.10, bf16[1,1024,256]{2,1,0:T(8,128)(2,1)S(1)} %copy-done.12), kind=kOutput, calls=%fused_computation.2 | convolution fusion | flops 2151153664 | bytes 19922944 | tf_op jit(solution)/shard_map/nbte,nde->btd/dot_general | solution.py:56
  205.9 0.0 reduce-scatter.5.cloned.1.call-update
  205.9 0.0 reduce-scatter.11.cloned.1.call-start
  206.0 1.1 copy-done.14
  207.1 6.5 %fusion.3 = f32[2,256,2048]{2,1,0:T(8,128)} fusion(bf16[2,1024,256]{2,1,0:T(8,128)(2,1)S(1)} %copy-done.14, bf16[1,1024,2048]{2,1,0:T(8,128)(2,1)} %all-gather.5.cloned.1.call-done), kind=kOutput, calls=%fused_computation.7 | convolution fusion | flops 2147483648 | bytes 9437184 | tf_op jit(solution)/shard_map/bhte,btd->hed/dot_general | solution.py:59
  213.7 0.0 reduce-scatter.11.cloned.1.call-update
  213.7 0.0 copy-start.1
  213.7 0.0 reduce-scatter.9.cloned.1.call-done
  213.7 2.0 slice_bitcast_fusion.11
  215.7 44.4 %reduce-scatter.7.cloned.1.call-done = f32[1024,2,256]{0,2,1:T(8,128)} async-done(((f32[2048,2,256]{0,2,1:T(8,128)}), f32[1024,2,256]{0,2,1:T(8,128)}) %reduce-scatter.7.cloned.1.call-update) | async-done | bytes 2097168 | tf_op jit(solution)/shard_map/reduce_scatter | solution.py:63
  260.1 4.1 %copy.34 = f32[1024,2,256]{2,1,0:T(2,128)} copy(f32[1024,2,256]{0,2,1:T(8,128)} %reduce-scatter.7.cloned.1.call-done) | data formatting | bytes 4194304
  264.2 63.4 %reduce-scatter.5.cloned.1.call-done = f32[1,256,2048]{2,1,0:T(8,128)} async-done(((f32[1,1024,2048]{2,1,0:T(8,128)}), f32[1,256,2048]{2,1,0:T(8,128)}) %reduce-scatter.5.cloned.1.call-update) | async-done | bytes 2097168 | tf_op jit(solution)/shard_map/reduce_scatter | solution.py:60
  327.6 2.7 convert_element_type.64
  330.3 51.5 %reduce-scatter.11.cloned.1.call-done = f32[2,256,1024]{2,1,0:T(8,128)} async-done(((f32[2,256,2048]{2,1,0:T(8,128)}), f32[2,256,1024]{2,1,0:T(8,128)}) %reduce-scatter.11.cloned.1.call-update) | async-done | bytes 2097168 | tf_op jit(solution)/shard_map/reduce_scatter | solution.py:64
  (36 shorter events, 0.1 us)
Async XLA Ops:
  7.2 36.7 %copy-start = (bf16[2,256,2048]{2,1,0:T(8,128)(2,1)S(1)}, bf16[2,256,2048]{2,1,0:T(8,128)(2,1)}, u32[]{:S(2)}) copy-start(bf16[2,256,2048]{2,1,0:T(8,128)(2,1)} %param.11) | copy-start | bytes 6291460
  7.2 36.7 %all-gather.5.cloned.1.call-start = ((), (), s32[]{:S(2)}) async-start(), calls=%async_computation.5 | async-start | bytes 5242880 | tf_op jit(solution)/shard_map/all_gather | solution.py:34
  7.9 69.0 %all-gather.3.cloned.1.call-start = ((), (), s32[]{:S(2)}) async-start(), calls=%async_computation.4 | async-start | bytes 5242880 | tf_op jit(solution)/shard_map/all_gather | solution.py:33
  8.7 205.1 %reduce-scatter.9.cloned.1.call-start = ((), (), s32[]{:S(2)}) async-start(), calls=%async_computation.8 | async-start | bytes 1572864 | tf_op jit(solution)/shard_map/reduce_scatter | solution.py:62
  10.3 73.0 %copy-start.5 = (bf16[1,2048,256]{1,2,0:T(8,128)(2,1)}, bf16[1,2048,256]{1,2,0:T(8,128)(2,1)S(1)}, u32[]{:S(2)}) copy-start(bf16[1,2048,256]{1,2,0:T(8,128)(2,1)S(1)} %copy.12) | copy-start | bytes 3145732
  52.0 31.3 %copy-start.7 = (bf16[1,2048,256]{1,2,0:T(8,128)(2,1)S(1)}, bf16[1,2048,256]{1,2,0:T(8,128)(2,1)}, u32[]{:S(2)}) copy-start(bf16[1,2048,256]{1,2,0:T(8,128)(2,1)} %copy.13) | copy-start | bytes 3145732
  76.9 6.3 %copy-start.2 = (bf16[1,1024,2048]{2,1,0:T(8,128)(2,1)S(1)}, bf16[1,1024,2048]{2,1,0:T(8,128)(2,1)}, u32[]{:S(2)}) copy-start(bf16[1,1024,2048]{2,1,0:T(8,128)(2,1)} %all-gather.3.cloned.1.call-done) | copy-start | bytes 12582916
  83.3 3.5 copy-start.17
  94.2 4.8 %copy-start.16 = (bf16[2,1024,256]{1,2,0:T(8,128)(2,1)S(1)}, bf16[2,1024,256]{1,2,0:T(8,128)(2,1)}, u32[]{:S(2)}) copy-start(bf16[2,1024,256]{1,2,0:T(8,128)(2,1)} %fusion.39) | copy-start | bytes 3145732
  94.2 9.2 %slice-start = ((s8[8388608]{0:T(1024)(128)(4,1)}), s8[4194304]{0:T(1024)(128)(4,1)S(1)}, s32[]{:S(2)}) async-start(s8[8388608]{0:T(1024)(128)(4,1)} %bitcast.131), calls=%async_computation.10 | async-start | bytes 8388608
  99.1 1.6 copy-start.13
  99.1 1.8 copy-start.18
  99.1 4.3 %slice-start.1 = ((s8[8388608]{0:T(1024)(128)(4,1)}), s8[4194304]{0:T(1024)(128)(4,1)S(1)}, s32[]{:S(2)}) async-start(s8[8388608]{0:T(1024)(128)(4,1)} %bitcast.131), calls=%async_computation.11 | async-start | bytes 8388608
  100.9 5.6 %copy-start.9 = (bf16[1,1024,256]{2,1,0:T(8,128)(2,1)}, bf16[1,1024,256]{2,1,0:T(8,128)(2,1)S(1)}, u32[]{:S(2)}) copy-start(bf16[1,1024,256]{2,1,0:T(8,128)(2,1)S(1)} %fusion.53) | copy-start | bytes 1572868
  103.4 1.7 copy-start.20
  105.2 2.1 copy-start.19
  105.2 3.7 copy-start.3
  108.9 4.5 %copy-start.11 = (bf16[1,1024,256]{2,1,0:T(8,128)(2,1)}, bf16[1,1024,256]{2,1,0:T(8,128)(2,1)S(1)}, u32[]{:S(2)}) copy-start(bf16[1,1024,256]{2,1,0:T(8,128)(2,1)S(1)} %fusion.54) | copy-start | bytes 1572868
  138.5 24.6 %collective-permute-start = (f32[2,512,256]{2,1,0:T(8,128)}, f32[2,512,256]{2,1,0:T(8,128)S(1)}, u32[]{:S(2)}, u32[]{:S(2)}) collective-permute-start(f32[2,512,256]{2,1,0:T(8,128)} %bitcast.135), channel_id=1, source_target_pairs={{0,1},{1,2},{2,3},{3,0},{4,5},{5,6},{6,7},{7,4}} | collective-permute-start | bytes 3145736 | tf_op jit(solution)/shard_map/ppermute | solution.py:19
  138.8 26.0 %collective-permute-start.1 = (f32[2,512,256]{2,1,0:T(8,128)}, f32[2,512,256]{2,1,0:T(8,128)}, u32[]{:S(2)}, u32[]{:S(2)}) collective-permute-start(f32[2,512,256]{2,1,0:T(8,128)} %bitcast.134), channel_id=1, source_target_pairs={{0,2},{1,3},{2,0},{3,1},{4,6},{5,7},{6,4},{7,5}} | collective-permute-start | bytes 3145736 | tf_op jit(solution)/shard_map/ppermute | solution.py:19
  139.2 45.2 %collective-permute-start.2 = (f32[2,512,256]{2,1,0:T(8,128)}, f32[2,512,256]{2,1,0:T(8,128)}, u32[]{:S(2)}, u32[]{:S(2)}) collective-permute-start(f32[2,512,256]{2,1,0:T(8,128)} %bitcast.133), channel_id=1, source_target_pairs={{0,3},{1,0},{2,1},{3,2},{4,7},{5,4},{6,5},{7,6}} | collective-permute-start | bytes 3145736 | tf_op jit(solution)/shard_map/ppermute | solution.py:19
  187.2 72.9 %reduce-scatter.7.cloned.1.call-start = ((), (), s32[]{:S(2)}) async-start(), calls=%async_computation.7 | async-start | bytes 6291456 | tf_op jit(solution)/shard_map/reduce_scatter | solution.py:63
  187.5 3.8 copy-start.4
  191.3 4.4 %copy-start.15 = (bf16[2,1024,256]{2,1,0:T(8,128)(2,1)}, bf16[2,1024,256]{2,1,0:T(8,128)(2,1)S(1)}, u32[]{:S(2)}) copy-start(bf16[2,1024,256]{2,1,0:T(8,128)(2,1)S(1)} %multiply_convert_fusion.1) | copy-start | bytes 3145732
  195.7 4.5 %copy-start.6 = (bf16[1,2048,256]{1,2,0:T(8,128)(2,1)S(1)}, bf16[1,2048,256]{1,2,0:T(8,128)(2,1)}, u32[]{:S(2)}) copy-start(bf16[1,2048,256]{1,2,0:T(8,128)(2,1)} %copy-done.5) | copy-start | bytes 3145732
  195.7 4.5 %copy-start.8 = (bf16[1,2048,256]{1,2,0:T(8,128)(2,1)S(1)}, bf16[1,2048,256]{1,2,0:T(8,128)(2,1)}, u32[]{:S(2)}) copy-start(bf16[1,2048,256]{1,2,0:T(8,128)(2,1)} %copy.13) | copy-start | bytes 3145732
  195.7 4.5 %copy-start.10 = (bf16[1,1024,256]{2,1,0:T(8,128)(2,1)S(1)}, bf16[1,1024,256]{2,1,0:T(8,128)(2,1)}, u32[]{:S(2)}) copy-start(bf16[1,1024,256]{2,1,0:T(8,128)(2,1)} %copy-done.9) | copy-start | bytes 1572868
  195.7 4.5 %copy-start.12 = (bf16[1,1024,256]{2,1,0:T(8,128)(2,1)S(1)}, bf16[1,1024,256]{2,1,0:T(8,128)(2,1)}, u32[]{:S(2)}) copy-start(bf16[1,1024,256]{2,1,0:T(8,128)(2,1)} %copy-done.11) | copy-start | bytes 1572868
  195.7 131.8 %reduce-scatter.5.cloned.1.call-start = ((), (), s32[]{:S(2)}) async-start(), calls=%async_computation.6 | async-start | bytes 10485760 | tf_op jit(solution)/shard_map/reduce_scatter | solution.py:60
  205.9 1.2 copy-start.14
  205.9 175.9 %reduce-scatter.11.cloned.1.call-start = ((), (), s32[]{:S(2)}) async-start(), calls=%async_computation.9 | async-start | bytes 6291456 | tf_op jit(solution)/shard_map/reduce_scatter | solution.py:64
  213.7 168.1 %copy-start.1 = (bf16[2,256,2048]{2,1,0:T(8,128)(2,1)S(1)}, bf16[2,256,2048]{2,1,0:T(8,128)(2,1)}, u32[]{:S(2)}) copy-start(bf16[2,256,2048]{2,1,0:T(8,128)(2,1)} %param.11) | copy-start | bytes 6291460
Sparse Core Ops, SparseCore 0:
  9.5 34.3 all-gather.4
  45.4 31.4 all-gather.2
  187.3 19.1 reduce-scatter.8
  208.5 51.5 reduce-scatter.6
  262.5 65.0 reduce-scatter.4
  330.3 51.5 reduce-scatter.10
where the time goes:
time: 389 us
  waiting for transfers between devices  258 us (66%)
  matrix products  58.8 us (15%)
  local copies, waits for them, and re-layouts  43.1 us (11%)
  between operations  14.5 us (4%)
  other arithmetic  11.6 us (3%)
    reduce_scatter x1, waiting for transfers between devices, device_step(): lax.psum_scatter(dx_part, 'model', scatter_dimension=1, tiled=True)  63.4 us
    reduce_scatter x1, waiting for transfers between devices, device_step(): lax.psum_scatter(dwo_part, 'data', scatter_dimension=2, tiled=True)  51.5 us
    reduce_scatter x1, waiting for transfers between devices, device_step(): lax.psum_scatter(dwq_part, 'data', scatter_dimension=0, tiled=True)  44.4 us
    ppermute x3, waiting for transfers between devices, subgroup_scatter_sum(): lax.ppermute(outgoing, 'model', subgroup_pairs(step_shift, sub_size, axis...  43 us
    all_gather x1, waiting for transfers between devices, device_step(): dy_full = lax.all_gather(dy_loc, 'model', axis=1, tiled=True)  29.7 us
    all_gather x1, waiting for transfers between devices, device_step(): x_full = lax.all_gather(x_loc, 'model', axis=1, tiled=True)  25 us
    unnamed x50, local copies, waits for them, and re-layouts  15 us
    dynamic_slice x2, local copies, waits for them, and re-layouts, subgroup_scatter_sum(): lax.dynamic_index_in_dim(row_blocks, my_slot, axis=1, keepdims=False)  12.3 us
  transfers between devices with their start and end apart: 9, of which 8 were waited for; matrix products, arithmetic and copies ran while one was open for 12% of the time, Pallas kernels for 0%

commit v1 on v0

v1 whole, which is shorter than its diff:
```python
import functools

import jax
import jax.numpy as jnp
from jax import lax
from jax.experimental import pallas as pl
from jax.experimental.pallas import tpu as pltpu
from jax.sharding import PartitionSpec as P

F32 = jnp.float32
BF16 = jnp.bfloat16
SEQ = 1024
BLK = 256
DIM = 2048
HD = 256
HEADS = 2
CH = 512
NCH = DIM // CH
HALF = DIM // 2
SCALE = HD ** -0.5
MESH = pl.DeviceIdType.MESH


def dot_nn(a, b):
    return lax.dot_general(a, b, (((1,), (0,)), ((), ())), preferred_element_type=F32)


def dot_nt(a, b):
    return lax.dot_general(a, b, (((1,), (1,)), ((), ())), preferred_element_type=F32)


def at(start, size, align=256):
    return pl.ds(pl.multiple_of(start, align), size)


def body(x_ref, dy_ref, wq_ref, wk_ref, wv_ref, wo_ref,
         dx_ref, dwq_ref, dwkv_ref, dwo_ref,
         xb, x_t, dyb, wq4, wkv, wo, q, k, v, k_t, v_t, p_t, o_t, do_acc, do_t,
         dkv, dkv_mate, dkv_send, dkv_part, dkv_full, dq, dq_mate,
         dwo_own, dwo_send, dwo_recv, dwq_own, dwq_send, dwq_recv,
         dx_own, dx_send, dx_recv, dx_out, dwkv_own, dwkv_send, dwkv_recv,
         sems, recvs, locs):
    model = lax.axis_index('model')
    data = lax.axis_index('data')
    chip = model // 2
    core = model % 2
    mate = {'model': chip * 2 + 1 - core}
    partner = {'model': (1 - chip) * 2 + core}
    peer = {'data': 1 - data}
    mate_row = (chip * 2 + 1 - core) * BLK
    own_row = model * BLK
    partner_row = ((1 - chip) * 2 + core) * BLK
    diag_row = ((1 - chip) * 2 + 1 - core) * BLK

    started = []
    slots = {}

    def slot(name):
        return slots.setdefault(name, len(slots))

    def send(name, src, dst, device):
        n = slot(name)
        copy = pltpu.make_async_remote_copy(src_ref=src, dst_ref=dst, send_sem=sems.at[n], recv_sem=recvs.at[n],
                                            device_id=device, device_id_type=MESH)
        copy.start()
        started.append(copy)

    def arrived(name, dst, device):
        n = slot(name)
        pltpu.make_async_remote_copy(src_ref=dst, dst_ref=dst, send_sem=sems.at[n], recv_sem=recvs.at[n],
                                     device_id=device, device_id_type=MESH).wait_recv()

    local_count = [0]

    def local(src, dst):
        copy = pltpu.make_async_copy(src, dst, locs.at[local_count[0]])
        local_count[0] += 1
        copy.start()
        return copy

    def chunk_at(j):
        return lax.rem((1 - data) * (NCH // 2) + j, NCH)

    barrier = pltpu.get_barrier_semaphore()
    for device in (mate, partner, peer):
        pl.semaphore_signal(barrier, inc=1, device_id=device, device_id_type=MESH)
    pl.semaphore_wait(barrier, 3)

    send('x_far', x_ref, xb.at[at(own_row, BLK)], partner)
    for j in range(NCH):
        c = chunk_at(j)
        send(f'dy_far{j}', dy_ref.at[:, at(c * CH, CH)], dyb.at[c, at(own_row, BLK)], partner)
    send('x_mate', x_ref, xb.at[at(own_row, BLK)], mate)
    loads = [local(x_ref, xb.at[at(own_row, BLK)]),
             local(wq_ref, wq4.at[pl.ds(core * HEADS, HEADS)]),
             local(wk_ref, wkv.at[0]), local(wv_ref, wkv.at[1])]
    late_loads = [local(wo_ref, wo)]
    for j in range(NCH):
        c = chunk_at(j)
        late_loads.append(local(dy_ref.at[:, at(c * CH, CH)], dyb.at[c, at(own_row, BLK)]))
        send(f'dy_mate{j}', dy_ref.at[:, at(c * CH, CH)], dyb.at[c, at(own_row, BLK)], mate)
    send('wq_mate', wq_ref, wq4.at[pl.ds(core * HEADS, HEADS)], mate)

    def project(first_row):
        def rows_step(r, carry):
            rows = at(first_row + r * BLK, BLK)
            xr = xb[rows, :]
            for h in range(HEADS):
                q[rows, h * HD:(h + 1) * HD] = dot_nn(xr, wq4[core * HEADS + h]).astype(BF16)
            kr = dot_nn(xr, wkv[0]).astype(BF16)
            vr = dot_nn(xr, wkv[1]).astype(BF16)
            k[rows, :] = kr
            v[rows, :] = vr
            k_t[:, rows] = kr.T
            v_t[:, rows] = vr.T

            def flip(t, inner):
                cols = at(t * 256, 256)
                x_t[cols, rows] = xb[rows, cols].T
                return inner
            lax.fori_loop(0, DIM // 256, flip, 0)
            return carry
        lax.fori_loop(0, 2, rows_step, 0)

    for copy in loads:
        copy.wait()
    arrived('x_mate', xb.at[at(mate_row, BLK)], mate)
    project(chip * 2 * BLK)

    arrived('x_far', xb.at[at(partner_row, BLK)], partner)
    send('x_fwd', xb.at[at(partner_row, BLK)], xb.at[at(partner_row, BLK)], mate)
    for copy in late_loads:
        copy.wait()
    for j in range(NCH):
        arrived(f'dy_mate{j}', dyb.at[chunk_at(j), at(mate_row, BLK)], mate)
    arrived('wq_mate', wq4.at[pl.ds((1 - core) * HEADS, HEADS)], mate)
    arrived('x_fwd', xb.at[at(diag_row, BLK)], mate)
    project((1 - chip) * 2 * BLK)

    def forward_chunk(j):
        c = chunk_at(j)
        block = dyb.at[c, at(partner_row, BLK)]
        arrived(f'dy_far{j}', block, partner)
        send(f'dy_fwd{j}', block, block, mate)

    mask = lax.broadcasted_iota(jnp.int32, (BLK, BLK), 0) <= lax.broadcasted_iota(jnp.int32, (BLK, BLK), 1)

    def forward_head(h, carry):
        heads = at(h * HD, HD)
        for i in range(SEQ // BLK):
            cols = slice(i * BLK, (i + 1) * BLK)
            qi = q[cols, heads]
            parts = []
            for j in range(i + 1):
                s = dot_nt(k[j * BLK:(j + 1) * BLK, :], qi) * SCALE
                parts.append(jnp.where(mask, s, -jnp.inf) if j == i else s)
            top = functools.reduce(jnp.maximum, [jnp.max(s, axis=0, keepdims=True) for s in parts])
            parts = [jnp.exp(s - top) for s in parts]
            total = functools.reduce(jnp.add, [jnp.sum(s, axis=0, keepdims=True) for s in parts])
            inv = 1.0 / total
            out = jnp.zeros((HD, BLK), F32)
            for j in range(i + 1):
                prob = parts[j] * inv
                p_t[h, j * BLK:(j + 1) * BLK, cols] = prob
                out += dot_nn(v_t[:, j * BLK:(j + 1) * BLK], prob.astype(BF16))
            o_t[heads, cols] = out.astype(BF16)
        return carry
    lax.fori_loop(0, HEADS, forward_head, 0)

    for j in range(NCH):
        c = chunk_at(j)
        forward_chunk(j)
        arrived(f'dy_fwd{j}', dyb.at[c, at(diag_row, BLK)], mate)
        part = dot_nt(wo[:, at(c * CH, CH)], dyb[c])
        if j == 0:
            do_acc[...] = part
        elif j < NCH - 1:
            do_acc[...] += part
        else:
            do_t[...] = (do_acc[...] + part).astype(BF16)
        if j < NCH // 2:
            dwo_send[j] = dot_nn(o_t[...], dyb[c]).astype(BF16)
            send(f'dwo{j}', dwo_send.at[j], dwo_recv.at[j], peer)

    dkv[...] = jnp.zeros(dkv.shape, F32)

    def backward_head(h, carry):
        heads = at(h * HD, HD)
        for i in range(SEQ // BLK):
            cols = slice(i * BLK, (i + 1) * BLK)
            qi = q[cols, heads]
            doi = do_t[heads, cols]
            delta = jnp.sum(doi.astype(F32) * o_t[heads, cols].astype(F32), axis=0, keepdims=True)
            dqi = jnp.zeros((HD, BLK), F32)
            for j in range(i + 1):
                rows = slice(j * BLK, (j + 1) * BLK)
                prob = p_t[h, rows, cols]
                ds = (prob * (dot_nn(v[rows, :], doi) - delta)).astype(BF16)
                dqi += dot_nn(k_t[:, rows], ds)
                dkv[0, rows, :] += dot_nn(ds, qi)
                dkv[1, rows, :] += dot_nt(prob.astype(BF16), doi)
            dq[h, cols, :] = (dqi * SCALE).astype(BF16).T
        return carry
    lax.fori_loop(0, HEADS, backward_head, 0)

    send('dkv_mate', dkv.at[1 - core], dkv_mate, mate)
    for b in range(2):
        rows = at((b * 2 + 1 - core) * BLK, BLK)
        send(f'dq_mate{b}', dq.at[:, rows], dq_mate.at[b], mate)
    arrived('dkv_mate', dkv_mate, mate)
    factor = jnp.where(core == 0, SCALE, 1.0).astype(F32)
    summed = (dkv[core] + dkv_mate[...]) * factor
    dkv_mate[...] = summed
    dkv_send[...] = summed.astype(BF16)
    send('dkv_far', dkv_send, dkv_part, partner)
    for b in range(2):
        arrived(f'dq_mate{b}', dq_mate.at[b], mate)

    def dx_cols(block, cols):
        rows = at((block * 2 + core) * BLK, BLK)
        acc = jnp.zeros((BLK, CH), F32)
        for h in range(HEADS):
            acc += dot_nt(dq[h, rows, :], wq4[core * HEADS + h, cols, :])
            acc += dot_nt(dq_mate[block, h], wq4[(1 - core) * HEADS + h, cols, :])
        return acc

    for j in range(NCH):
        dx_send[j] = dx_cols(1 - chip, slice(j * CH, (j + 1) * CH)).astype(BF16)
        send(f'dx{j}', dx_send.at[j], dx_recv.at[j], partner)

    def dwq_step(r, carry):
        rows = at((1 - data) * HALF + r * 256, 256)
        for h in range(HEADS):
            dwq_send[h, at(r * 256, 256), :] = dot_nn(x_t[rows, :], dq[h]).astype(BF16)
        return carry
    lax.fori_loop(0, HALF // 256, dwq_step, 0)
    send('dwq', dwq_send, dwq_recv, peer)

    def dwq_own_step(r, carry):
        rows = at(data * HALF + r * 256, 256)
        for h in range(HEADS):
            dwq_own[h, at(r * 256, 256), :] = dot_nn(x_t[rows, :], dq[h])
        return carry
    lax.fori_loop(0, HALF // 256, dwq_own_step, 0)

    for j in range(NCH):
        dx_own[:, j * CH:(j + 1) * CH] = dx_cols(chip, slice(j * CH, (j + 1) * CH))
    for j in range(NCH // 2, NCH):
        dwo_own[:, (j - NCH // 2) * CH:(j - NCH // 2 + 1) * CH] = dot_nn(o_t[...], dyb[chunk_at(j)])

    arrived('dkv_far', dkv_part, partner)
    dkv_full[core] = (dkv_mate[...] + dkv_part[...].astype(F32)).astype(BF16)
    send('dkv_full', dkv_full.at[core], dkv_full.at[core], mate)
    for j in range(NCH // 2):
        arrived(f'dwo{j}', dwo_recv.at[j], peer)
        dwo_own[:, j * CH:(j + 1) * CH] += dwo_recv[j].astype(F32)
    outs = []
    outs.append(local(dwo_own, dwo_ref))
    arrived('dkv_full', dkv_full.at[1 - core], mate)
    for n in range(2):
        peer_rows = at((model * 2 + 1 - data) * 256, 256)
        dwkv_send[n] = dot_nn(x_t[peer_rows, :], dkv_full[n]).astype(BF16)
    send('dwkv', dwkv_send, dwkv_recv, peer)
    for n in range(2):
        dwkv_own[n] = dot_nn(x_t[at((model * 2 + data) * 256, 256), :], dkv_full[n])
    for j in range(NCH):
        cols = slice(j * CH, (j + 1) * CH)
        dx_own[:, cols] += (dot_nt(dkv_full[0, at(own_row, BLK), :], wkv[0, cols, :])
                            + dot_nt(dkv_full[1, at(own_row, BLK), :], wkv[1, cols, :]))

    arrived('dwq', dwq_recv, peer)

    def dwq_sum(r, carry):
        rows = at(r * 256, 256)
        for h in range(HEADS):
            dwq_own[h, rows, :] += dwq_recv[h, rows, :].astype(F32)
        return carry
    lax.fori_loop(0, HALF // 256, dwq_sum, 0)
    outs.append(local(dwq_own, dwq_ref))
    arrived('dwkv', dwkv_recv, peer)
    for n in range(2):
        dwkv_own[n] += dwkv_recv[n].astype(F32)
    outs.append(local(dwkv_own, dwkv_ref))
    for j in range(NCH):
        arrived(f'dx{j}', dx_recv.at[j], partner)
        cols = slice(j * CH, (j + 1) * CH)
        dx_out[:, cols] = (dx_own[:, cols] + dx_recv[j].astype(F32)).astype(BF16)
    outs.append(local(dx_out, dx_ref))
    for copy in started:
        copy.wait_send()
    for copy in outs:
        copy.wait()
    assert len(slots) <= sems.shape[0] and local_count[0] <= locs.shape[0]


def fused_step(x, dy, wq, wk, wv, wo):
    any_spec = pl.BlockSpec(memory_space=pl.ANY)
    scratch = [
        pltpu.VMEM((SEQ, DIM), BF16),
        pltpu.VMEM((DIM, SEQ), BF16),
        pltpu.VMEM((NCH, SEQ, CH), BF16),
        pltpu.VMEM((2 * HEADS, DIM, HD), BF16),
        pltpu.VMEM((2, DIM, HD), BF16),
        pltpu.VMEM((HEADS * HD, DIM), BF16),
        pltpu.VMEM((SEQ, HEADS * HD), BF16),
        pltpu.VMEM((SEQ, HD), BF16),
        pltpu.VMEM((SEQ, HD), BF16),
        pltpu.VMEM((HD, SEQ), BF16),
        pltpu.VMEM((HD, SEQ), BF16),
        pltpu.VMEM((HEADS, SEQ, SEQ), F32),
        pltpu.VMEM((HEADS * HD, SEQ), BF16),
        pltpu.VMEM((HEADS * HD, SEQ), F32),
        pltpu.VMEM((HEADS * HD, SEQ), BF16),
        pltpu.VMEM((2, SEQ, HD), F32),
        pltpu.VMEM((SEQ, HD), F32),
        pltpu.VMEM((SEQ, HD), BF16),
        pltpu.VMEM((SEQ, HD), BF16),
        pltpu.VMEM((2, SEQ, HD), BF16),
        pltpu.VMEM((HEADS, SEQ, HD), BF16),
        pltpu.VMEM((2, HEADS, BLK, HD), BF16),
        pltpu.VMEM((HEADS * HD, HALF), F32),
        pltpu.VMEM((NCH // 2, HEADS * HD, CH), BF16),
        pltpu.VMEM((NCH // 2, HEADS * HD, CH), BF16),
        pltpu.VMEM((HEADS, HALF, HD), F32),
        pltpu.VMEM((HEADS, HALF, HD), BF16),
        pltpu.VMEM((HEADS, HALF, HD), BF16),
        pltpu.VMEM((BLK, DIM), F32),
        pltpu.VMEM((NCH, BLK, CH), BF16),
        pltpu.VMEM((NCH, BLK, CH), BF16),
        pltpu.VMEM((BLK, DIM), BF16),
        pltpu.VMEM((2, 256, HD), F32),
        pltpu.VMEM((2, 256, HD), BF16),
        pltpu.VMEM((2, 256, HD), BF16),
        pltpu.SemaphoreType.DMA((32,)),
        pltpu.SemaphoreType.DMA((32,)),
        pltpu.SemaphoreType.DMA((16,)),
    ]
    return pl.pallas_call(
        body,
        out_shape=(jax.ShapeDtypeStruct((BLK, DIM), BF16),
                   jax.ShapeDtypeStruct((HEADS, HALF, HD), F32),
                   jax.ShapeDtypeStruct((2, 256, HD), F32),
                   jax.ShapeDtypeStruct((HEADS * HD, HALF), F32)),
        in_specs=[any_spec] * 6,
        out_specs=(any_spec,) * 4,
        scratch_shapes=scratch,
        compiler_params=pltpu.CompilerParams(collective_id=0, has_side_effects=True,
                                             vmem_limit_bytes=67_043_328),
        name='attention_backward',
    )(x, dy, wq, wk, wv, wo)


def solution(mesh):
    tok_spec = P(('pod', 'data'), 'model', None)

    def device_step(x_loc, dy_loc, w_q, w_k, w_v, w_o):
        dx, dwq, dwkv, dwo = fused_step(x_loc[0], dy_loc[0], jnp.transpose(w_q, (1, 0, 2)), w_k[0], w_v[0],
                                        w_o.reshape(HEADS * HD, DIM))
        return (dx[None], jnp.transpose(dwq, (1, 0, 2)), dwkv[0], dwkv[1], dwo.reshape(HEADS, HD, HALF))

    kv_rows = P(('pod', 'model', 'data'), None)
    return jax.shard_map(device_step, mesh=mesh,
                         in_specs=(tok_spec, tok_spec, P(None, 'model', None), P(), P(), P('model', None, None)),
                         out_specs=(tok_spec, P(('pod', 'data'), 'model', None), kv_rows, kv_rows,
                                    P(('pod', 'model'), None, 'data')),
                         check_vma=False)
```

time: 389 us -> 107 us (0.28)
  waiting for transfers between devices: 258 us -> 0 us
  Pallas kernels: 0 us -> 95.6 us
  matrix products: 58.8 us -> 0 us
  local copies, waits for them, and re-layouts: 43.1 us -> 11 us
  between operations: 14.5 us -> 0.66 us
  other arithmetic: 11.6 us -> 0 us
    reduce_scatter x4 -> x0, waiting for transfers between devices: 159 us -> none  [the longest x1 63.4 us: device_step(): lax.psum_scatter(dx_part, 'model', scatter_dimension=1, tiled=True)]
    pallas_call x0 -> x1, Pallas kernels: none -> 95.6 us  [fused_step(): pl.pallas_call(body, out_shape=(jax.ShapeDtypeStruct((BLK, DIM), BF16), j...]
    all_gather x2 -> x0, waiting for transfers between devices: 54.6 us -> none  [the longest x1 29.7 us: device_step(): dy_full = lax.all_gather(dy_loc, 'model', axis=1, tiled=True)]
    dot_general x13 -> x0, matrix products: 51.4 us -> none  [the longest x1 6.52 us: device_step(): jnp.einsum('bhte,btd->hed', out_loc, dy_full, preferred_element_type=jnp....]
    ppermute x3 -> x0, waiting for transfers between devices: 43 us -> none  [subgroup_scatter_sum(): lax.ppermute(outgoing, 'model', subgroup_pairs(step_shift, sub_size, axis...]
    dynamic_slice x5 -> x0, local copies, waits for them, and re-layouts: 20.1 us -> none  [the longest x2 12.3 us: subgroup_scatter_sum(): lax.dynamic_index_in_dim(row_blocks, my_slot, axis=1, keepdims=False)]
    convert_element_type x2 -> x0, other arithmetic: 7.52 us -> none  [the longest x1 4.81 us: device_step(): prob_bf = attn_prob.astype(jnp.bfloat16)]
    sub x1 -> x0, matrix products: 7.45 us -> none  [device_step(): attn_prob = jax.nn.softmax(jnp.where(causal, scores, -jnp.inf), axis=-1)]
  transfers between devices with their start and end apart: 9 -> 0, of which waited for: 8 -> 0; matrix products, arithmetic and copies ran while one was open for 12% -> 0% of each run, Pallas kernels for 0% -> 0%
where the time goes in v1:
time: 107 us
  Pallas kernels  95.6 us (89%)
  local copies, waits for them, and re-layouts  11 us (10%)
    pallas_call x1, Pallas kernels, fused_step(): pl.pallas_call(body, out_shape=(jax.ShapeDtypeStruct((BLK, DIM), BF16), j...  95.6 us
    unnamed x10, local copies, waits for them, and re-layouts  10.1 us

profile of v1, /device:TPU:0, one launch (start us, length us, event | category | flops | bytes accessed | tf_op | source)
XLA Modules:
  0.0 107.2 jit_solution(16148123122777155786)
XLA Ops:
  0.6 3.2 %copy.14 = bf16[2048,2,256]{2,0,1:T(8,128)(2,1)} copy(bf16[2048,2,256]{2,1,0:T(2,128)(2,1)} %param.8) | data formatting | bytes 4194304 | tf_op args[2]
  3.8 95.6 %attention_backward.1 = (bf16[256,2048]{1,0:T(8,128)(2,1)}, f32[2,1024,256]{2,1,0:T(8,128)}, f32[2,256,256]{2,1,0:T(8,128)}, f32[512,1024]{1,0:T(8,128)}) custom-call(bf16[256,2048]{1,0:T(8,128)(2,1)} %bitcast.20, bf16[256,2048]{1,0:T(8,128)(2,1)} %bitcast.21, bf16[2,2048,256]{2,1,0:T(8,128)(2,1)} %bitcast.15, bf16[2048,256]{1,0:T(8,128)(2,1)} %bitcast.22, ...), custom_call_target="tpu_custom_call" | custom-call | tf_op jit(solution)/shard_map/attention_backward/pallas_call | solution.py:338
  99.4 0.0 copy-start.2
  99.4 0.0 copy-start.1
  99.4 4.6 %copy.12 = f32[1024,2,256]{2,1,0:T(2,128)} copy(f32[1024,2,256]{2,0,1:T(8,128)} %bitcast.17) | data formatting | bytes 4194304
  104.1 0.0 copy-done.2
  104.1 0.0 copy-start
  104.1 0.8 slice_bitcast_fusion
  104.9 0.0 copy-done.1
  104.9 1.0 copy.17
  105.9 0.0 copy-done
  105.9 1.3 %copy.18 = f32[2,256,1024]{2,1,0:T(8,128)} copy(f32[2,256,1024]{2,1,0:T(8,128)S(1)} %bitcast.16) | data formatting | bytes 4194304
Async XLA Ops:
  99.4 4.7 %copy-start.2 = (f32[2,256,256]{2,1,0:T(8,128)S(1)}, f32[2,256,256]{2,1,0:T(8,128)}, u32[]{:S(2)}) copy-start(f32[2,256,256]{2,1,0:T(8,128)} %get-tuple-element.11) | copy-start | bytes 1572868
  99.4 5.5 %copy-start.1 = (bf16[256,2048]{1,0:T(8,128)(2,1)S(1)}, bf16[256,2048]{1,0:T(8,128)(2,1)}, u32[]{:S(2)}) copy-start(bf16[256,2048]{1,0:T(8,128)(2,1)} %get-tuple-element.9) | copy-start | bytes 3145732
  104.1 1.8 %copy-start = (f32[512,1024]{1,0:T(8,128)S(1)}, f32[512,1024]{1,0:T(8,128)}, u32[]{:S(2)}) copy-start(f32[512,1024]{1,0:T(8,128)} %get-tuple-element.12) | copy-start | bytes 6291460

commit v2 on v1

v2 whole, which is shorter than its diff:
```python
import functools

import jax
import jax.numpy as jnp
from jax import lax
from jax.experimental import pallas as pl
from jax.experimental.pallas import tpu as pltpu
from jax.sharding import PartitionSpec as P

F32 = jnp.float32
BF16 = jnp.bfloat16
SEQ = 1024
BLK = 256
DIM = 2048
HD = 256
HEADS = 2
CH = 512
NCH = DIM // CH
PIECE = 64
NP = BLK // PIECE
HALF = DIM // 2
SCALE = HD ** -0.5
MESH = pl.DeviceIdType.MESH


def dot_nn(a, b):
    return lax.dot_general(a, b, (((1,), (0,)), ((), ())), preferred_element_type=F32)


def dot_nt(a, b):
    return lax.dot_general(a, b, (((1,), (1,)), ((), ())), preferred_element_type=F32)


def at(start, size, align=256):
    return pl.ds(pl.multiple_of(start, align), size)


def body(x_ref, dy_ref, wq_ref, wk_ref, wv_ref, wo_ref,
         dx_out, dwq_out, dwk_out, dwv_out, dwo_out,
         xb, x_t, dyb, wq_raw, wq4, wkv, wo, q, k, v, k_t, v_t, p_t, ds_t, o_t, do_acc, do_t,
         dkv, dkv_mate, dkv_send, dkv_part, dkv_full, dq, dq_mate,
         dwo_send, dwo_recv, dwq_send, dwq_recv,
         dx_own, dx_send, dx_recv, dwkv_send, dwkv_recv,
         sems, recvs, locs):
    model = lax.axis_index('model')
    data = lax.axis_index('data')
    chip = model // 2
    core = model % 2
    mate = {'model': chip * 2 + 1 - core}
    partner = {'model': (1 - chip) * 2 + core}
    peer = {'data': 1 - data}
    own_row = model * BLK
    mate_row = (chip * 2 + 1 - core) * BLK
    partner_row = ((1 - chip) * 2 + core) * BLK
    diag_row = ((1 - chip) * 2 + 1 - core) * BLK
    near = chip * 2 * BLK
    far = (1 - chip) * 2 * BLK

    started = []
    slots = {}

    def slot(name):
        return slots.setdefault(name, len(slots))

    def send(name, src, dst, device):
        n = slot(name)
        copy = pltpu.make_async_remote_copy(src_ref=src, dst_ref=dst, send_sem=sems.at[n], recv_sem=recvs.at[n],
                                            device_id=device, device_id_type=MESH)
        copy.start()
        started.append(copy)

    def arrived(name, dst, device):
        n = slot(name)
        with jax.named_scope('w_' + name):
            pltpu.make_async_remote_copy(src_ref=dst, dst_ref=dst, send_sem=sems.at[n], recv_sem=recvs.at[n],
                                         device_id=device, device_id_type=MESH).wait_recv()

    local_count = [0]

    def local(src, dst):
        copy = pltpu.make_async_copy(src, dst, locs.at[local_count[0]])
        local_count[0] += 1
        copy.start()
        return copy

    def chunk_at(j):
        return lax.rem((1 - data) * (NCH // 2) + j, NCH)

    def x_piece(row, p):
        return at(row + p * PIECE, PIECE, PIECE)

    def send_dy(j):
        c = chunk_at(j)
        send(f'dy_far{j}', dy_ref.at[:, at(c * CH, CH)], dyb.at[c, at(own_row, BLK)], partner)

    barrier = pltpu.get_barrier_semaphore()
    for device in (mate, partner, peer):
        pl.semaphore_signal(barrier, inc=1, device_id=device, device_id_type=MESH)
    loads = [local(x_ref, xb.at[at(own_row, BLK)]), local(wq_ref, wq_raw),
             local(wk_ref, wkv.at[0]), local(wv_ref, wkv.at[1])]
    with jax.named_scope('barrier'):
        pl.semaphore_wait(barrier, 3)

    for p in range(NP):
        send(f'x_far{p}', x_ref.at[pl.ds(p * PIECE, PIECE)], xb.at[x_piece(own_row, p)], partner)
    send('x_mate', x_ref, xb.at[at(own_row, BLK)], mate)
    late_loads = [local(wo_ref, wo)]
    for j in range(NCH):
        c = chunk_at(j)
        late_loads.append(local(dy_ref.at[:, at(c * CH, CH)], dyb.at[c, at(own_row, BLK)]))
        send(f'dy_mate{j}', dy_ref.at[:, at(c * CH, CH)], dyb.at[c, at(own_row, BLK)], mate)

    def project(xr, pieces):
        def put(dst, lo, value):
            for row, size, off in pieces:
                dst[row, lo:lo + HD] = value[off:off + size]
        for h in range(HEADS):
            put(q, h * HD, dot_nn(xr, wq4[core * HEADS + h]).astype(BF16))
        for n, (dst, dst_t) in enumerate(((k, k_t), (v, v_t))):
            value = dot_nn(xr, wkv[n]).astype(BF16)
            put(dst, 0, value)

    def flip_x(first_row):
        def step(t, carry):
            cols = at(t * 256, 256)
            for r in range(2):
                rows = at(first_row + r * BLK, BLK)
                x_t[cols, rows] = xb[rows, cols].T
            return carry
        lax.fori_loop(0, DIM // 256, step, 0)

    def flip_kv(first_row):
        for r in range(2):
            rows = at(first_row + r * BLK, BLK)
            k_t[:, rows] = k[rows, :].T
            v_t[:, rows] = v[rows, :].T

    with jax.named_scope('loads'):
        for copy in loads:
            copy.wait()

    with jax.named_scope('relay'):
        def relay(r, carry):
            rows = at(r * 128, 128, 128)
            for h in range(HEADS):
                wq4[core * HEADS + h, rows, :] = wq_raw[rows, h, :]
            return carry
        lax.fori_loop(0, DIM // 128, relay, 0)
    send('wq_mate', wq4.at[pl.ds(core * HEADS, HEADS)], wq4.at[pl.ds(core * HEADS, HEADS)], mate)

    arrived('x_mate', xb.at[at(mate_row, BLK)], mate)
    with jax.named_scope('proj1'):
        def project_near(r, carry):
            rows = at(near + r * BLK, BLK)
            project(xb[rows, :], [(rows, BLK, 0)])
            return carry
        lax.fori_loop(0, 2, project_near, 0)
        flip_kv(near)

    def forward_x(p):
        block = xb.at[x_piece(partner_row, p)]
        arrived(f'x_far{p}', block, partner)
        send(f'x_fwd{p}', block, block, mate)

    def project_far(p):
        for n in (p - 1, p):
            arrived(f'x_fwd{n}', xb.at[x_piece(diag_row, n)], mate)
        first = (p - 1) * PIECE
        rows = [at(row + first, 2 * PIECE, PIECE) for row in (partner_row, diag_row)]
        xr = jnp.concatenate([xb[r, :] for r in rows], axis=0)
        with jax.named_scope('proj2'):
            project(xr, [(rows[0], 2 * PIECE, 0), (rows[1], 2 * PIECE, 2 * PIECE)])

    forward_x(0)
    with jax.named_scope('flip1'):
        flip_x(near)
    forward_x(1)
    send_dy(0)
    project_far(1)
    for copy in late_loads:
        copy.wait()
    for j in range(NCH):
        arrived(f'dy_mate{j}', dyb.at[chunk_at(j), at(mate_row, BLK)], mate)
    with jax.named_scope('do_near'):
        for half in range(HEADS):
            heads = slice(half * HD, (half + 1) * HD)
            acc = jnp.zeros((HD, 2 * BLK), F32)
            for c in range(NCH):
                acc += dot_nt(wo[heads, c * CH:(c + 1) * CH], dyb[c, at(near, 2 * BLK), :])
            do_t[heads, at(near, 2 * BLK)] = acc.astype(BF16)
        dkv[...] = jnp.zeros(dkv.shape, F32)
    forward_x(2)
    send_dy(1)
    forward_x(3)
    send_dy(2)
    send_dy(3)
    project_far(3)
    flip_kv(far)

    mask = lax.broadcasted_iota(jnp.int32, (BLK, BLK), 0) <= lax.broadcasted_iota(jnp.int32, (BLK, BLK), 1)

    def forward_head(h, carry):
        heads = at(h * HD, HD)
        for i in range(SEQ // BLK):
            cols = slice(i * BLK, (i + 1) * BLK)
            qi = q[cols, heads]
            parts = []
            for j in range(i + 1):
                s = dot_nt(k[j * BLK:(j + 1) * BLK, :], qi) * SCALE
                parts.append(jnp.where(mask, s, -jnp.inf) if j == i else s)
            top = functools.reduce(jnp.maximum, [jnp.max(s, axis=0, keepdims=True) for s in parts])
            parts = [jnp.exp(s - top) for s in parts]
            total = functools.reduce(jnp.add, [jnp.sum(s, axis=0, keepdims=True) for s in parts])
            inv = 1.0 / total
            out = jnp.zeros((HD, BLK), F32)
            for j in range(i + 1):
                prob = parts[j] * inv
                p_t[h, j * BLK:(j + 1) * BLK, cols] = prob
                out += dot_nn(v_t[:, j * BLK:(j + 1) * BLK], prob.astype(BF16))
            o_t[heads, cols] = out.astype(BF16)
        return carry
    with jax.named_scope('fwd'):
        lax.fori_loop(0, HEADS, forward_head, 0)

    def add_dkv(h, i, j, prob, ds):
        rows = slice(j * BLK, (j + 1) * BLK)
        cols = slice(i * BLK, (i + 1) * BLK)
        heads = at(h * HD, HD)
        dkv[0, rows, :] += dot_nn(ds, q[cols, heads])
        dkv[1, rows, :] += dot_nt(prob.astype(BF16), do_t[heads, cols])

    def backward_block(h, i, keep):
        heads = at(h * HD, HD)
        cols = slice(i * BLK, (i + 1) * BLK)
        doi = do_t[heads, cols]
        delta = jnp.sum(doi.astype(F32) * o_t[heads, cols].astype(F32), axis=0, keepdims=True)
        dqi = jnp.zeros((HD, BLK), F32)
        for j in range(i + 1):
            rows = slice(j * BLK, (j + 1) * BLK)
            prob = p_t[h, rows, cols]
            ds = (prob * (dot_nn(v[rows, :], doi) - delta)).astype(BF16)
            dqi += dot_nn(k_t[:, rows], ds)
            if keep:
                ds_t[h, rows, (i % 2) * BLK:(i % 2 + 1) * BLK] = ds
            else:
                add_dkv(h, i, j, prob, ds)
        dq[h, cols, :] = (dqi * SCALE).astype(BF16).T

    def over_heads(step):
        def one(h, carry):
            step(h)
            return carry
        lax.fori_loop(0, HEADS, one, 0)

    def take_chunk(j):
        c = chunk_at(j)
        block = dyb.at[c, at(partner_row, BLK)]
        arrived(f'dy_far{j}', block, partner)
        send(f'dy_fwd{j}', block, block, mate)
        arrived(f'dy_fwd{j}', dyb.at[c, at(diag_row, BLK)], mate)
        part = dot_nt(wo[:, at(c * CH, CH)], dyb[c, at(far, 2 * BLK), :])
        if j == 0:
            do_acc[...] = part
        elif j < NCH - 1:
            do_acc[...] += part
        else:
            do_t[:, at(far, 2 * BLK)] = (do_acc[...] + part).astype(BF16)
        if j < NCH // 2:
            dwo_send[j] = dot_nn(o_t[...], dyb[c]).astype(BF16)
            send(f'dwo{j}', dwo_send.at[j], dwo_recv.at[j], peer)

    take_chunk(0)
    take_chunk(1)

    for c in range(2):
        @pl.when(chip == c)
        def _(c=c):
            def step(h):
                for i in (2 * c, 2 * c + 1):
                    backward_block(h, i, False)
            with jax.named_scope('bwd_near'):
                over_heads(step)
    send('dq_near', dq.at[:, at(mate_row, BLK)], dq_mate.at[chip], mate)
    take_chunk(2)
    with jax.named_scope('flip2'):
        flip_x(far)
    take_chunk(3)

    for c in range(2):
        for first in range(2):
            @pl.when((chip == c) & (core == 1 - first))
            def _(c=c, first=first):
                with jax.named_scope('bwd_far0'):
                    over_heads(lambda h: backward_block(h, 2 * (1 - c) + first, True))
    send('dq_far', dq.at[:, at(diag_row, BLK)], dq_mate.at[1 - chip], mate)
    for c in range(2):
        for first in range(2):
            @pl.when((chip == c) & (core == 1 - first))
            def _(c=c, first=first):
                with jax.named_scope('bwd_far1'):
                    over_heads(lambda h: backward_block(h, 2 * (1 - c) + 1 - first, True))
    arrived('wq_mate', wq4.at[pl.ds((1 - core) * HEADS, HEADS)], mate)
    arrived('dq_far', dq_mate.at[1 - chip], mate)

    def dx_cols(block, cols):
        rows = at((block * 2 + core) * BLK, BLK)
        acc = jnp.zeros((BLK, CH), F32)
        for h in range(HEADS):
            acc += dot_nt(dq[h, rows, :], wq4[core * HEADS + h, cols, :])
            acc += dot_nt(dq_mate[block, h], wq4[(1 - core) * HEADS + h, cols, :])
        return acc

    def send_dx(j):
        dx_send[j] = dx_cols(1 - chip, slice(j * CH, (j + 1) * CH)).astype(BF16)
        send(f'dx{j}', dx_send.at[j], dx_recv.at[j], partner)

    send_dx(0)
    send_dx(1)
    for c in range(2):
        @pl.when(chip == c)
        def _(c=c):
            def step(h):
                for i in (2 * (1 - c), 2 * (1 - c) + 1):
                    for j in range(i + 1):
                        rows = slice(j * BLK, (j + 1) * BLK)
                        add_dkv(h, i, j, p_t[h, rows, i * BLK:(i + 1) * BLK],
                                ds_t[h, rows, (i % 2) * BLK:(i % 2 + 1) * BLK])
            with jax.named_scope('dkv'):
                over_heads(step)
    send('dkv_mate', dkv.at[1 - core], dkv_mate, mate)

    def send_dwq(r):
        with jax.named_scope('dwq'):
            rows = at((1 - data) * HALF + r * 256, 256)
            for h in range(HEADS):
                dwq_send[r, h] = dot_nn(x_t[rows, :], dq[h]).astype(BF16)
            send(f'dwq{r}', dwq_send.at[r], dwq_recv.at[r], peer)
    send_dwq(0)
    arrived('dkv_mate', dkv_mate, mate)
    factor = jnp.where(core == 0, SCALE, 1.0).astype(F32)
    summed = (dkv[core] + dkv_mate[...]) * factor
    dkv_mate[...] = summed
    dkv_send[...] = summed.astype(BF16)
    send('dkv_far', dkv_send, dkv_part, partner)
    send_dx(2)
    send_dx(3)
    for r in range(1, 4):
        send_dwq(r)

    arrived('dq_near', dq_mate.at[chip], mate)
    for j in range(NCH):
        dx_own[:, j * CH:(j + 1) * CH] = dx_cols(chip, slice(j * CH, (j + 1) * CH))
    for j in range(NCH // 2):
        arrived(f'dwo{j}', dwo_recv.at[j], peer)
        cols = slice(j * CH, (j + 1) * CH)
        dwo_out[:, cols] = dot_nn(o_t[...], dyb[chunk_at(NCH // 2 + j)]) + dwo_recv[j].astype(F32)

    arrived('dkv_far', dkv_part, partner)
    dkv_full[core] = (dkv_mate[...] + dkv_part[...].astype(F32)).astype(BF16)
    send('dkv_full', dkv_full.at[core], dkv_full.at[core], mate)
    arrived('dkv_full', dkv_full.at[1 - core], mate)
    for n in range(2):
        peer_rows = at((model * 2 + 1 - data) * 256, 256)
        dwkv_send[n] = dot_nn(x_t[peer_rows, :], dkv_full[n]).astype(BF16)
    send('dwkv', dwkv_send, dwkv_recv, peer)
    kept_rows = at((model * 2 + data) * 256, 256)
    dwk_out[...] = dot_nn(x_t[kept_rows, :], dkv_full[0])
    dwv_out[...] = dot_nn(x_t[kept_rows, :], dkv_full[1])
    for j in range(NCH):
        cols = slice(j * CH, (j + 1) * CH)
        dx_own[:, cols] += (dot_nt(dkv_full[0, at(own_row, BLK), :], wkv[0, cols, :])
                            + dot_nt(dkv_full[1, at(own_row, BLK), :], wkv[1, cols, :]))

    def finish_dx(j):
        arrived(f'dx{j}', dx_recv.at[j], partner)
        cols = slice(j * CH, (j + 1) * CH)
        dx_out[:, cols] = (dx_own[:, cols] + dx_recv[j].astype(F32)).astype(BF16)

    finish_dx(0)
    finish_dx(1)
    for r in range(4):
        arrived(f'dwq{r}', dwq_recv.at[r], peer)
        with jax.named_scope('dwq_sum'):
            rows = at(data * HALF + r * 256, 256)
            for h in range(HEADS):
                value = dot_nn(x_t[rows, :], dq[h]) + dwq_recv[r, h].astype(F32)
                dwq_out[r * 256:(r + 1) * 256, h, :] = value
    finish_dx(2)
    arrived('dwkv', dwkv_recv, peer)
    dwk_out[...] += dwkv_recv[0].astype(F32)
    dwv_out[...] += dwkv_recv[1].astype(F32)
    finish_dx(3)
    with jax.named_scope('sends'):
        for copy in started:
            copy.wait_send()
    assert len(slots) <= sems.shape[0] and local_count[0] <= locs.shape[0]


def fused_step(x, dy, wq, wk, wv, wo):
    any_spec = pl.BlockSpec(memory_space=pl.ANY)
    vmem_spec = pl.BlockSpec(memory_space=pltpu.VMEM)
    scratch = [
        pltpu.VMEM((SEQ, DIM), BF16),
        pltpu.VMEM((DIM, SEQ), BF16),
        pltpu.VMEM((NCH, SEQ, CH), BF16),
        pltpu.VMEM((DIM, HEADS, HD), BF16),
        pltpu.VMEM((2 * HEADS, DIM, HD), BF16),
        pltpu.VMEM((2, DIM, HD), BF16),
        pltpu.VMEM((HEADS * HD, DIM), BF16),
        pltpu.VMEM((SEQ, HEADS * HD), BF16),
        pltpu.VMEM((SEQ, HD), BF16),
        pltpu.VMEM((SEQ, HD), BF16),
        pltpu.VMEM((HD, SEQ), BF16),
        pltpu.VMEM((HD, SEQ), BF16),
        pltpu.VMEM((HEADS, SEQ, SEQ), F32),
        pltpu.VMEM((HEADS, SEQ, 2 * BLK), BF16),
        pltpu.VMEM((HEADS * HD, SEQ), BF16),
        pltpu.VMEM((HEADS * HD, 2 * BLK), F32),
        pltpu.VMEM((HEADS * HD, SEQ), BF16),
        pltpu.VMEM((2, SEQ, HD), F32),
        pltpu.VMEM((SEQ, HD), F32),
        pltpu.VMEM((SEQ, HD), BF16),
        pltpu.VMEM((SEQ, HD), BF16),
        pltpu.VMEM((2, SEQ, HD), BF16),
        pltpu.VMEM((HEADS, SEQ, HD), BF16),
        pltpu.VMEM((2, HEADS, BLK, HD), BF16),
        pltpu.VMEM((NCH // 2, HEADS * HD, CH), BF16),
        pltpu.VMEM((NCH // 2, HEADS * HD, CH), BF16),
        pltpu.VMEM((4, HEADS, HALF // 4, HD), BF16),
        pltpu.VMEM((4, HEADS, HALF // 4, HD), BF16),
        pltpu.VMEM((BLK, DIM), F32),
        pltpu.VMEM((NCH, BLK, CH), BF16),
        pltpu.VMEM((NCH, BLK, CH), BF16),
        pltpu.VMEM((2, 256, HD), BF16),
        pltpu.VMEM((2, 256, HD), BF16),
        pltpu.SemaphoreType.DMA((48,)),
        pltpu.SemaphoreType.DMA((48,)),
        pltpu.SemaphoreType.DMA((16,)),
    ]
    return pl.pallas_call(
        body,
        out_shape=(pltpu.VMEM((BLK, DIM), BF16),
                   pltpu.VMEM((HALF, HEADS, HD), F32),
                   pltpu.VMEM((256, HD), F32),
                   pltpu.VMEM((256, HD), F32),
                   pltpu.VMEM((HEADS * HD, HALF), F32)),
        in_specs=[any_spec] * 6,
        out_specs=(vmem_spec,) * 5,
        scratch_shapes=scratch,
        compiler_params=pltpu.CompilerParams(collective_id=0, has_side_effects=True,
                                             vmem_limit_bytes=58 * 2 ** 20),
        name='attention_backward',
    )(x, dy, wq, wk, wv, wo)


def solution(mesh):
    tok_spec = P(('pod', 'data'), 'model', None)

    def device_step(x_loc, dy_loc, w_q, w_k, w_v, w_o):
        dx, dwq, dwk, dwv, dwo = fused_step(x_loc[0], dy_loc[0], w_q, w_k[0], w_v[0],
                                            w_o.reshape(HEADS * HD, DIM))
        return dx[None], dwq, dwk, dwv, dwo.reshape(HEADS, HD, HALF)

    kv_rows = P(('pod', 'model', 'data'), None)
    return jax.shard_map(device_step, mesh=mesh,
                         in_specs=(tok_spec, tok_spec, P(None, 'model', None), P(), P(), P('model', None, None)),
                         out_specs=(tok_spec, P(('pod', 'data'), 'model', None), kv_rows, kv_rows,
                                    P(('pod', 'model'), None, 'data')),
                         check_vma=False)
```

time: 107 us -> 96.9 us (0.906)
  local copies, waits for them, and re-layouts: 11 us -> 5.01 us
  Pallas kernels: 95.6 us -> 91.2 us
    unnamed x10 -> x5, local copies, waits for them, and re-layouts: 10.1 us -> 5.01 us
    pallas_call x1, Pallas kernels: 95.6 us -> 91.2 us  [fused_step(): pl.pallas_call(body, out_shape=(pltpu.VMEM((BLK, DIM), BF16), pltpu.VMEM(...]
where the time goes in v2:
time: 96.9 us; the launch traced here: 96.8 us
  Pallas kernels  91.2 us (94%)
  local copies, waits for them, and re-layouts  5.01 us (5%)
    pallas_call x1, Pallas kernels, fused_step(): pl.pallas_call(body, out_shape=(pltpu.VMEM((BLK, DIM), BF16), pltpu.VMEM(...  91.2 us
    unnamed x5, local copies, waits for them, and re-layouts  5.01 us

profile of v2, /device:TPU:0, one launch (start us, length us, event | category | flops | bytes accessed | tf_op | source)
XLA Modules:
  0.0 96.8 jit_solution(4987250122209019310)
XLA Ops:
  0.6 91.2 %attention_backward.1 = (bf16[256,2048]{1,0:T(8,128)(2,1)S(1)}, f32[1024,2,256]{2,1,0:T(2,128)S(1)}, f32[256,256]{1,0:T(8,128)S(1)}, f32[256,256]{1,0:T(8,128)S(1)}, f32[512,1024]{1,0:T(8,128)S(1)}) custom-call(bf16[256,2048]{1,0:T(8,128)(2,1)} %bitcast.10, bf16[256,2048]{1,0:T(8,128)(2,1)} %bitcast.11, bf16[2048,2,256]{2,1,0:T(2,128)(2,1)} %wq_ref.1, ...), custom_call_target="tpu_custom_call" | custom-call | tf_op jit(solution)/shard_map/attention_backward/pallas_call | solution.py:440
  91.8 1.0 %copy.16 = bf16[1,256,2048]{2,1,0:T(8,128)(2,1)} copy(bf16[1,256,2048]{2,1,0:T(8,128)(2,1)S(1)} %bitcast.8) | data formatting | bytes 2097152
  92.8 0.7 copy.18
  93.5 0.7 copy.19
  94.2 1.3 %copy.17 = f32[1024,2,256]{2,1,0:T(2,128)} copy(f32[1024,2,256]{2,1,0:T(2,128)S(1)} %get-tuple-element.16) | data formatting | bytes 4194304
  95.5 1.3 %copy.20 = f32[2,256,1024]{2,1,0:T(8,128)} copy(f32[2,256,1024]{2,1,0:T(8,128)S(1)} %bitcast.7) | data formatting | bytes 4194304

commit v3 on v2

--- a/solution.py
+++ b/solution.py
@@ -14,8 +14,10 @@
 DIM = 2048
 HD = 256
 HEADS = 2
-CH = 512
+CH = 256
 NCH = DIM // CH
+DXC = 512
+NDX = DIM // DXC
 PIECE = 64
 NP = BLK // PIECE
 HALF = DIM // 2
@@ -56,30 +58,32 @@
     near = chip * 2 * BLK
     far = (1 - chip) * 2 * BLK
 
-    started = []
+    groups = {}
     slots = {}
-
-    def slot(name):
-        return slots.setdefault(name, len(slots))
-
-    def send(name, src, dst, device):
-        n = slot(name)
-        copy = pltpu.make_async_remote_copy(src_ref=src, dst_ref=dst, send_sem=sems.at[n], recv_sem=recvs.at[n],
-                                            device_id=device, device_id_type=MESH)
+    devices = {}
+
+    def send(name, src, dst, device, group=None, part=None):
+        group = group or name
+        devices[group] = device
+        copy = pltpu.make_async_remote_copy(
+            src_ref=src, dst_ref=dst, send_sem=sems.at[groups.setdefault(group, len(groups))],
+            recv_sem=recvs.at[slots.setdefault(part or name, len(slots))],
+            device_id=device, device_id_type=MESH)
         copy.start()
-        started.append(copy)
 
     def arrived(name, dst, device):
-        n = slot(name)
         with jax.named_scope('w_' + name):
-            pltpu.make_async_remote_copy(src_ref=dst, dst_ref=dst, send_sem=sems.at[n], recv_sem=recvs.at[n],
-                                         device_id=device, device_id_type=MESH).wait_recv()
-
-    local_count = [0]
-
-    def local(src, dst):
-        copy = pltpu.make_async_copy(src, dst, locs.at[local_count[0]])
-        local_count[0] += 1
+            pltpu.make_async_remote_copy(
+                src_ref=dst, dst_ref=dst, send_sem=sems.at[0],
+                recv_sem=recvs.at[slots.setdefault(name, len(slots))],
+                device_id=device, device_id_type=MESH).wait_recv()
+
+    def sent(group, src):
+        pltpu.make_async_remote_copy(src_ref=src, dst_ref=src, send_sem=sems.at[groups[group]], recv_sem=recvs.at[0],
+                                     device_id=devices[group], device_id_type=MESH).wait_send()
+
+    def local(src, dst, n):
+        copy = pltpu.make_async_copy(src, dst, locs.at[n])
         copy.start()
         return copy
 
@@ -91,24 +95,24 @@
 
     def send_dy(j):
         c = chunk_at(j)
-        send(f'dy_far{j}', dy_ref.at[:, at(c * CH, CH)], dyb.at[c, at(own_row, BLK)], partner)
+        send(f'dy_far{j}', dy_ref.at[:, at(c * CH, CH)], dyb.at[c, at(own_row, BLK)], partner, 'dy_far')
 
     barrier = pltpu.get_barrier_semaphore()
     for device in (mate, partner, peer):
         pl.semaphore_signal(barrier, inc=1, device_id=device, device_id_type=MESH)
-    loads = [local(x_ref, xb.at[at(own_row, BLK)]), local(wq_ref, wq_raw),
-             local(wk_ref, wkv.at[0]), local(wv_ref, wkv.at[1])]
+    loads = [local(x_ref, xb.at[at(own_row, BLK)], 0), local(wq_ref, wq_raw, 1),
+             local(wk_ref, wkv.at[0], 2), local(wv_ref, wkv.at[1], 3)]
     with jax.named_scope('barrier'):
         pl.semaphore_wait(barrier, 3)
 
     for p in range(NP):
-        send(f'x_far{p}', x_ref.at[pl.ds(p * PIECE, PIECE)], xb.at[x_piece(own_row, p)], partner)
+        send(f'x_far{p}', x_ref.at[pl.ds(p * PIECE, PIECE)], xb.at[x_piece(own_row, p)], partner, 'x_far')
     send('x_mate', x_ref, xb.at[at(own_row, BLK)], mate)
-    late_loads = [local(wo_ref, wo)]
-    for j in range(NCH):
-        c = chunk_at(j)
-        late_loads.append(local(dy_ref.at[:, at(c * CH, CH)], dyb.at[c, at(own_row, BLK)]))
-        send(f'dy_mate{j}', dy_ref.at[:, at(c * CH, CH)], dyb.at[c, at(own_row, BLK)], mate)
+    late_load = local(wo_ref, wo, 4)
+    for c in range(NCH):
+        own_chunk = dyb.at[c, at(own_row, BLK)]
+        local(dy_ref.at[:, c * CH:(c + 1) * CH], own_chunk, 5)
+        send('dy_mate', dy_ref.at[:, c * CH:(c + 1) * CH], own_chunk, mate)
 
     def project(xr, pieces):
         def put(dst, lo, value):
@@ -160,12 +164,11 @@
     def forward_x(p):
         block = xb.at[x_piece(partner_row, p)]
         arrived(f'x_far{p}', block, partner)
-        send(f'x_fwd{p}', block, block, mate)
+        send(f'x_fwd{p}', block, block, mate, 'x_fwd', f'x_fwd{p | 1}')
 
     def project_far(p):
-        for n in (p - 1, p):
-            arrived(f'x_fwd{n}', xb.at[x_piece(diag_row, n)], mate)
         first = (p - 1) * PIECE
+        arrived(f'x_fwd{p}', xb.at[at(diag_row + first, 2 * PIECE, PIECE)], mate)
         rows = [at(row + first, 2 * PIECE, PIECE) for row in (partner_row, diag_row)]
         xr = jnp.concatenate([xb[r, :] for r in rows], axis=0)
         with jax.named_scope('proj2'):
@@ -175,12 +178,11 @@
     with jax.named_scope('flip1'):
         flip_x(near)
     forward_x(1)
-    send_dy(0)
     project_far(1)
-    for copy in late_loads:
-        copy.wait()
-    for j in range(NCH):
-        arrived(f'dy_mate{j}', dyb.at[chunk_at(j), at(mate_row, BLK)], mate)
+    late_load.wait()
+    own_dy = dyb.at[:, at(own_row, BLK)]
+    pltpu.make_async_copy(own_dy, own_dy, locs.at[5]).wait()
+    arrived('dy_mate', dyb.at[:, at(mate_row, BLK)], mate)
     with jax.named_scope('do_near'):
         for half in range(HEADS):
             heads = slice(half * HD, (half + 1) * HD)
@@ -190,17 +192,22 @@
             do_t[heads, at(near, 2 * BLK)] = acc.astype(BF16)
         dkv[...] = jnp.zeros(dkv.shape, F32)
     forward_x(2)
-    send_dy(1)
+    for j in range(NCH):
+        send_dy(j)
     forward_x(3)
-    send_dy(2)
-    send_dy(3)
     project_far(3)
     flip_kv(far)
 
+    def forward_dy(j):
+        block = dyb.at[chunk_at(j), at(partner_row, BLK)]
+        arrived(f'dy_far{j}', block, partner)
+        send(f'dy_fwd{j}', block, block, mate, 'dy_fwd')
+
+    forward_dy(0)
     mask = lax.broadcasted_iota(jnp.int32, (BLK, BLK), 0) <= lax.broadcasted_iota(jnp.int32, (BLK, BLK), 1)
 
     def forward_head(h, carry):
-        heads = at(h * HD, HD)
+        heads = slice(h * HD, (h + 1) * HD) if isinstance(h, int) else at(h * HD, HD)
         for i in range(SEQ // BLK):
             cols = slice(i * BLK, (i + 1) * BLK)
             qi = q[cols, heads]
@@ -220,17 +227,18 @@
             o_t[heads, cols] = out.astype(BF16)
         return carry
     with jax.named_scope('fwd'):
-        lax.fori_loop(0, HEADS, forward_head, 0)
+        for h in range(HEADS):
+            forward_head(h, 0)
 
     def add_dkv(h, i, j, prob, ds):
         rows = slice(j * BLK, (j + 1) * BLK)
         cols = slice(i * BLK, (i + 1) * BLK)
-        heads = at(h * HD, HD)
+        heads = slice(h * HD, (h + 1) * HD) if isinstance(h, int) else at(h * HD, HD)
         dkv[0, rows, :] += dot_nn(ds, q[cols, heads])
         dkv[1, rows, :] += dot_nt(prob.astype(BF16), do_t[heads, cols])
 
     def backward_block(h, i, keep):
-        heads = at(h * HD, HD)
+        heads = slice(h * HD, (h + 1) * HD) if isinstance(h, int) else at(h * HD, HD)
         cols = slice(i * BLK, (i + 1) * BLK)
         doi = do_t[heads, cols]
         delta = jnp.sum(doi.astype(F32) * o_t[heads, cols].astype(F32), axis=0, keepdims=True)
@@ -254,9 +262,6 @@
 
     def take_chunk(j):
         c = chunk_at(j)
-        block = dyb.at[c, at(partner_row, BLK)]
-        arrived(f'dy_far{j}', block, partner)
-        send(f'dy_fwd{j}', block, block, mate)
         arrived(f'dy_fwd{j}', dyb.at[c, at(diag_row, BLK)], mate)
         part = dot_nt(wo[:, at(c * CH, CH)], dyb[c, at(far, 2 * BLK), :])
         if j == 0:
@@ -267,10 +272,14 @@
             do_t[:, at(far, 2 * BLK)] = (do_acc[...] + part).astype(BF16)
         if j < NCH // 2:
             dwo_send[j] = dot_nn(o_t[...], dyb[c]).astype(BF16)
-            send(f'dwo{j}', dwo_send.at[j], dwo_recv.at[j], peer)
-
+            send(f'dwo{j}', dwo_send.at[j], dwo_recv.at[j], peer, 'dwo')
+
+    forward_dy(1)
     take_chunk(0)
+    forward_dy(2)
     take_chunk(1)
+    take_chunk(2)
+    forward_dy(3)
 
     for c in range(2):
         @pl.when(chip == c)
@@ -280,39 +289,47 @@
                     backward_block(h, i, False)
             with jax.named_scope('bwd_near'):
                 over_heads(step)
-    send('dq_near', dq.at[:, at(mate_row, BLK)], dq_mate.at[chip], mate)
-    take_chunk(2)
+    send('dq_near', dq.at[:, at(mate_row, BLK)], dq_mate.at[chip], mate, 'dq')
+    forward_dy(4)
+    take_chunk(3)
+    forward_dy(5)
+    take_chunk(4)
+    take_chunk(5)
     with jax.named_scope('flip2'):
         flip_x(far)
-    take_chunk(3)
+    for j in range(6, NCH):
+        forward_dy(j)
+        take_chunk(j)
 
     for c in range(2):
         for first in range(2):
             @pl.when((chip == c) & (core == 1 - first))
             def _(c=c, first=first):
                 with jax.named_scope('bwd_far0'):
-                    over_heads(lambda h: backward_block(h, 2 * (1 - c) + first, True))
-    send('dq_far', dq.at[:, at(diag_row, BLK)], dq_mate.at[1 - chip], mate)
+                    for h in range(HEADS):
+                        backward_block(h, 2 * (1 - c) + first, True)
+    send('dq_far', dq.at[:, at(diag_row, BLK)], dq_mate.at[1 - chip], mate, 'dq')
     for c in range(2):
         for first in range(2):
             @pl.when((chip == c) & (core == 1 - first))
             def _(c=c, first=first):
                 with jax.named_scope('bwd_far1'):
-                    over_heads(lambda h: backward_block(h, 2 * (1 - c) + 1 - first, True))
+                    for h in range(HEADS):
+                        backward_block(h, 2 * (1 - c) + 1 - first, True)
     arrived('wq_mate', wq4.at[pl.ds((1 - core) * HEADS, HEADS)], mate)
     arrived('dq_far', dq_mate.at[1 - chip], mate)
 
     def dx_cols(block, cols):
         rows = at((block * 2 + core) * BLK, BLK)
-        acc = jnp.zeros((BLK, CH), F32)
+        acc = jnp.zeros((BLK, DXC), F32)
         for h in range(HEADS):
             acc += dot_nt(dq[h, rows, :], wq4[core * HEADS + h, cols, :])
             acc += dot_nt(dq_mate[block, h], wq4[(1 - core) * HEADS + h, cols, :])
         return acc
 
     def send_dx(j):
-        dx_send[j] = dx_cols(1 - chip, slice(j * CH, (j + 1) * CH)).astype(BF16)
-        send(f'dx{j}', dx_send.at[j], dx_recv.at[j], partner)
+        dx_send[j] = dx_cols(1 - chip, slice(j * DXC, (j + 1) * DXC)).astype(BF16)
+        send(f'dx{j}', dx_send.at[j], dx_recv.at[j], partner, 'dx')
 
     send_dx(0)
     send_dx(1)
@@ -334,7 +351,7 @@
             rows = at((1 - data) * HALF + r * 256, 256)
             for h in range(HEADS):
                 dwq_send[r, h] = dot_nn(x_t[rows, :], dq[h]).astype(BF16)
-            send(f'dwq{r}', dwq_send.at[r], dwq_recv.at[r], peer)
+            send(f'dwq{r}', dwq_send.at[r], dwq_recv.at[r], peer, 'dwq')
     send_dwq(0)
     arrived('dkv_mate', dkv_mate, mate)
     factor = jnp.where(core == 0, SCALE, 1.0).astype(F32)
@@ -348,8 +365,8 @@
         send_dwq(r)
 
     arrived('dq_near', dq_mate.at[chip], mate)
-    for j in range(NCH):
-        dx_own[:, j * CH:(j + 1) * CH] = dx_cols(chip, slice(j * CH, (j + 1) * CH))
+    for j in range(NDX):
+        dx_own[:, j * DXC:(j + 1) * DXC] = dx_cols(chip, slice(j * DXC, (j + 1) * DXC))
     for j in range(NCH // 2):
         arrived(f'dwo{j}', dwo_recv.at[j], peer)
         cols = slice(j * CH, (j + 1) * CH)
@@ -366,14 +383,14 @@
     kept_rows = at((model * 2 + data) * 256, 256)
     dwk_out[...] = dot_nn(x_t[kept_rows, :], dkv_full[0])
     dwv_out[...] = dot_nn(x_t[kept_rows, :], dkv_full[1])
-    for j in range(NCH):
-        cols = slice(j * CH, (j + 1) * CH)
+    for j in range(NDX):
+        cols = slice(j * DXC, (j + 1) * DXC)
         dx_own[:, cols] += (dot_nt(dkv_full[0, at(own_row, BLK), :], wkv[0, cols, :])
                             + dot_nt(dkv_full[1, at(own_row, BLK), :], wkv[1, cols, :]))
 
     def finish_dx(j):
         arrived(f'dx{j}', dx_recv.at[j], partner)
-        cols = slice(j * CH, (j + 1) * CH)
+        cols = slice(j * DXC, (j + 1) * DXC)
         dx_out[:, cols] = (dx_own[:, cols] + dx_recv[j].astype(F32)).astype(BF16)
 
     finish_dx(0)
@@ -391,9 +408,22 @@
     dwv_out[...] += dwkv_recv[1].astype(F32)
     finish_dx(3)
     with jax.named_scope('sends'):
-        for copy in started:
-            copy.wait_send()
-    assert len(slots) <= sems.shape[0] and local_count[0] <= locs.shape[0]
+        sent('x_far', x_ref)
+        sent('x_mate', x_ref)
+        sent('dy_far', dy_ref)
+        sent('dy_mate', dy_ref)
+        sent('wq_mate', wq4.at[pl.ds(core * HEADS, HEADS)])
+        sent('x_fwd', xb.at[at(partner_row, BLK)])
+        sent('dy_fwd', dyb.at[:, at(partner_row, BLK)])
+        sent('dwo', dwo_send)
+        sent('dq', dq_mate)
+        sent('dx', dx_send)
+        sent('dkv_mate', dkv_mate)
+        sent('dkv_far', dkv_send)
+        sent('dkv_full', dkv_send)
+        sent('dwq', dwq_send)
+        sent('dwkv', dwkv_send)
+    assert len(groups) == sems.shape[0] and len(slots) == recvs.shape[0]
 
 
 def fused_step(x, dy, wq, wk, wv, wo):
@@ -429,13 +459,13 @@
         pltpu.VMEM((4, HEADS, HALF // 4, HD), BF16),
         pltpu.VMEM((4, HEADS, HALF // 4, HD), BF16),
         pltpu.VMEM((BLK, DIM), F32),
-        pltpu.VMEM((NCH, BLK, CH), BF16),
-        pltpu.VMEM((NCH, BLK, CH), BF16),
+        pltpu.VMEM((NDX, BLK, DXC), BF16),
+        pltpu.VMEM((NDX, BLK, DXC), BF16),
         pltpu.VMEM((2, 256, HD), BF16),
         pltpu.VMEM((2, 256, HD), BF16),
-        pltpu.SemaphoreType.DMA((48,)),
-        pltpu.SemaphoreType.DMA((48,)),
-        pltpu.SemaphoreType.DMA((16,)),
+        pltpu.SemaphoreType.DMA((15,)),
+        pltpu.SemaphoreType.DMA((43,)),
+        pltpu.SemaphoreType.DMA((6,)),
     ]
     return pl.pallas_call(
         body,
@@ -453,12 +483,34 @@
     )(x, dy, wq, wk, wv, wo)
 
 
+def flush_body(*refs):
+    sources, results, sems = refs[:5], refs[5:10], refs[10]
+    copies = [pltpu.make_async_copy(a, b, sems.at[n]) for n, (a, b) in enumerate(zip(sources, results))]
+    for copy in copies:
+        copy.start()
+    for copy in copies:
+        copy.wait()
+
+
+def flush(*arrays):
+    any_spec = pl.BlockSpec(memory_space=pl.ANY)
+    return pl.pallas_call(
+        flush_body,
+        out_shape=tuple(jax.ShapeDtypeStruct(a.shape, a.dtype) for a in arrays),
+        in_specs=[any_spec] * 5,
+        out_specs=(any_spec,) * 5,
+        scratch_shapes=[pltpu.SemaphoreType.DMA((5,))],
+        compiler_params=pltpu.CompilerParams(vmem_limit_bytes=2 ** 20),
+        name='write_results',
+    )(*arrays)
+
+
 def solution(mesh):
     tok_spec = P(('pod', 'data'), 'model', None)
 
     def device_step(x_loc, dy_loc, w_q, w_k, w_v, w_o):
-        dx, dwq, dwk, dwv, dwo = fused_step(x_loc[0], dy_loc[0], w_q, w_k[0], w_v[0],
-                                            w_o.reshape(HEADS * HD, DIM))
+        dx, dwq, dwk, dwv, dwo = flush(*fused_step(x_loc[0], dy_loc[0], w_q, w_k[0], w_v[0],
+                                                   w_o.reshape(HEADS * HD, DIM)))
         return dx[None], dwq, dwk, dwv, dwo.reshape(HEADS, HD, HALF)
 
     kv_rows = P(('pod', 'model', 'data'), None)

time: 96.9 us -> 93.5 us (0.965)
  local copies, waits for them, and re-layouts: 5.01 us -> 0 us
  Pallas kernels: 91.2 us -> 92.6 us
    unnamed x5 -> x0, local copies, waits for them, and re-layouts: 5.01 us -> none
    pallas_call x0 -> x1, Pallas kernels: none -> 2.57 us  [flush(): pl.pallas_call(flush_body, out_shape=tuple((jax.ShapeDtypeStruct(a.shape,...]
    pallas_call x1, Pallas kernels: 91.2 us -> 90 us  [fused_step(): pl.pallas_call(body, out_shape=(pltpu.VMEM((BLK, DIM), BF16), pltpu.VMEM(...]
where the time goes in v3:
time: 93.5 us; the launch traced here: 93.4 us
  Pallas kernels  92.6 us (99%)
    pallas_call x1, Pallas kernels, fused_step(): pl.pallas_call(body, out_shape=(pltpu.VMEM((BLK, DIM), BF16), pltpu.VMEM(...  90 us
    pallas_call x1, Pallas kernels, flush(): pl.pallas_call(flush_body, out_shape=tuple((jax.ShapeDtypeStruct(a.shape,...  2.57 us

profile of v3, /device:TPU:0, one launch (start us, length us, event | category | flops | bytes accessed | tf_op | source)
XLA Modules:
  0.0 93.4 jit_solution(17253472627797764407)
XLA Ops:
  0.6 90.0 %attention_backward.1 = (bf16[256,2048]{1,0:T(8,128)(2,1)S(1)}, f32[1024,2,256]{2,1,0:T(2,128)S(1)}, f32[256,256]{1,0:T(8,128)S(1)}, f32[256,256]{1,0:T(8,128)S(1)}, f32[512,1024]{1,0:T(8,128)S(1)}) custom-call(bf16[256,2048]{1,0:T(8,128)(2,1)} %bitcast.8, bf16[256,2048]{1,0:T(8,128)(2,1)} %bitcast.9, bf16[2048,2,256]{2,1,0:T(2,128)(2,1)} %wq_ref.1, ...), custom_call_target="tpu_custom_call" | custom-call | tf_op jit(solution)/shard_map/attention_backward/pallas_call | solution.py:470
  90.7 2.6 %write_results.1 = (bf16[256,2048]{1,0:T(8,128)(2,1)}, f32[1024,2,256]{2,1,0:T(2,128)}, f32[256,256]{1,0:T(8,128)}, f32[256,256]{1,0:T(8,128)}, f32[512,1024]{1,0:T(8,128)}) custom-call(bf16[256,2048]{1,0:T(8,128)(2,1)S(1)} %get-tuple-element.15.refs_0_, f32[1024,2,256]{2,1,0:T(2,128)S(1)} %get-tuple-element.16.refs_1_, ...), custom_call_target="tpu_custom_call" | custom-call | tf_op jit(solution)/shard_map/write_results/pallas_call | solution.py:497

commit v4 on v3

--- a/solution.py
+++ b/solution.py
@@ -18,6 +18,7 @@
 NCH = DIM // CH
 DXC = 512
 NDX = DIM // DXC
+GRP = 128
 PIECE = 64
 NP = BLK // PIECE
 HALF = DIM // 2
@@ -39,7 +40,7 @@
 
 def body(x_ref, dy_ref, wq_ref, wk_ref, wv_ref, wo_ref,
          dx_out, dwq_out, dwk_out, dwv_out, dwo_out,
-         xb, x_t, dyb, wq_raw, wq4, wkv, wo, q, k, v, k_t, v_t, p_t, ds_t, o_t, do_acc, do_t,
+         xb, x_t, dyb, wq_raw, wq4, wkv, wo, q, k, v, k_t, v_t, p_t, p_inv, ds_t, o_t, do_acc, do_t,
          dkv, dkv_mate, dkv_send, dkv_part, dkv_full, dq, dq_mate,
          dwo_send, dwo_recv, dwq_send, dwq_recv,
          dx_own, dx_send, dx_recv, dwkv_send, dwkv_recv,
@@ -93,9 +94,20 @@
     def x_piece(row, p):
         return at(row + p * PIECE, PIECE, PIECE)
 
-    def send_dy(j):
-        c = chunk_at(j)
-        send(f'dy_far{j}', dy_ref.at[:, at(c * CH, CH)], dyb.at[c, at(own_row, BLK)], partner, 'dy_far')
+    late = pl.ds(data * (NCH // 2), NCH // 2)
+
+    def group_row(row, g):
+        return at(row + g * GRP, GRP, GRP)
+
+    def send_dy():
+        for j in range(NCH // 2):
+            c = chunk_at(j)
+            send(f'dy_far{j}', dy_ref.at[:, at(c * CH, CH)], dyb.at[c, at(own_row, BLK)], partner, 'dy_far')
+        for g in range(2):
+            for j in range(NCH // 2):
+                c = data * (NCH // 2) + j
+                send(f'dy_late{g}', dy_ref.at[g * GRP:(g + 1) * GRP, at(c * CH, CH)],
+                     dyb.at[c, group_row(own_row, g)], partner, 'dy_far')
 
     barrier = pltpu.get_barrier_semaphore()
     for device in (mate, partner, peer):
@@ -164,15 +176,15 @@
     def forward_x(p):
         block = xb.at[x_piece(partner_row, p)]
         arrived(f'x_far{p}', block, partner)
-        send(f'x_fwd{p}', block, block, mate, 'x_fwd', f'x_fwd{p | 1}')
+        send(f'x_fwd{p}', block, block, mate, 'x_fwd', f'x_fwd{max(p, 1)}')
 
     def project_far(p):
-        first = (p - 1) * PIECE
-        arrived(f'x_fwd{p}', xb.at[at(diag_row + first, 2 * PIECE, PIECE)], mate)
-        rows = [at(row + first, 2 * PIECE, PIECE) for row in (partner_row, diag_row)]
+        first, size = (0, 2 * PIECE) if p == 1 else (p * PIECE, PIECE)
+        arrived(f'x_fwd{p}', xb.at[at(diag_row + first, size, PIECE)], mate)
+        rows = [at(row + first, size, PIECE) for row in (partner_row, diag_row)]
         xr = jnp.concatenate([xb[r, :] for r in rows], axis=0)
         with jax.named_scope('proj2'):
-            project(xr, [(rows[0], 2 * PIECE, 0), (rows[1], 2 * PIECE, 2 * PIECE)])
+            project(xr, [(rows[0], size, 0), (rows[1], size, size)])
 
     forward_x(0)
     with jax.named_scope('flip1'):
@@ -192,9 +204,16 @@
             do_t[heads, at(near, 2 * BLK)] = acc.astype(BF16)
         dkv[...] = jnp.zeros(dkv.shape, F32)
     forward_x(2)
-    for j in range(NCH):
-        send_dy(j)
+
+    @pl.when(core == 0)
+    def _():
+        send_dy()
+    project_far(2)
     forward_x(3)
+
+    @pl.when(core == 1)
+    def _():
+        send_dy()
     project_far(3)
     flip_kv(far)
 
@@ -203,53 +222,52 @@
         arrived(f'dy_far{j}', block, partner)
         send(f'dy_fwd{j}', block, block, mate, 'dy_fwd')
 
-    forward_dy(0)
     mask = lax.broadcasted_iota(jnp.int32, (BLK, BLK), 0) <= lax.broadcasted_iota(jnp.int32, (BLK, BLK), 1)
 
-    def forward_head(h, carry):
-        heads = slice(h * HD, (h + 1) * HD) if isinstance(h, int) else at(h * HD, HD)
-        for i in range(SEQ // BLK):
-            cols = slice(i * BLK, (i + 1) * BLK)
-            qi = q[cols, heads]
-            parts = []
-            for j in range(i + 1):
-                s = dot_nt(k[j * BLK:(j + 1) * BLK, :], qi) * SCALE
-                parts.append(jnp.where(mask, s, -jnp.inf) if j == i else s)
-            top = functools.reduce(jnp.maximum, [jnp.max(s, axis=0, keepdims=True) for s in parts])
-            parts = [jnp.exp(s - top) for s in parts]
-            total = functools.reduce(jnp.add, [jnp.sum(s, axis=0, keepdims=True) for s in parts])
-            inv = 1.0 / total
-            out = jnp.zeros((HD, BLK), F32)
-            for j in range(i + 1):
-                prob = parts[j] * inv
-                p_t[h, j * BLK:(j + 1) * BLK, cols] = prob
-                out += dot_nn(v_t[:, j * BLK:(j + 1) * BLK], prob.astype(BF16))
-            o_t[heads, cols] = out.astype(BF16)
-        return carry
+    def forward_block(h, i):
+        heads = slice(h * HD, (h + 1) * HD)
+        cols = slice(i * BLK, (i + 1) * BLK)
+        rows = (i + 1) * BLK
+        qs = q[cols, heads] * jnp.asarray(SCALE, BF16)
+        p_t[h, i * BLK:rows, cols] = jnp.where(mask, dot_nt(k[i * BLK:rows, :], qs), -jnp.inf)
+        if i:
+            p_t[h, :i * BLK, cols] = dot_nt(k[:i * BLK, :], qs)
+        top = jnp.max(p_t[h, :rows, cols], axis=0, keepdims=True)
+        e = jnp.exp(p_t[h, :rows, cols] - top)
+        p_t[h, :rows, cols] = e
+        inv = 1.0 / jnp.sum(e, axis=0, keepdims=True)
+        p_inv[h, :, cols] = inv
+        prob = (p_t[h, :rows, cols] * inv).astype(BF16)
+        o_t[heads, cols] = dot_nn(v_t[:, :rows], prob).astype(BF16)
     with jax.named_scope('fwd'):
+        for i in range(3):
+            for h in range(HEADS):
+                forward_block(h, i)
+        forward_dy(0)
         for h in range(HEADS):
-            forward_head(h, 0)
+            forward_block(h, 3)
 
     def add_dkv(h, i, j, prob, ds):
         rows = slice(j * BLK, (j + 1) * BLK)
         cols = slice(i * BLK, (i + 1) * BLK)
-        heads = slice(h * HD, (h + 1) * HD) if isinstance(h, int) else at(h * HD, HD)
+        heads = at(h * HD, HD)
         dkv[0, rows, :] += dot_nn(ds, q[cols, heads])
         dkv[1, rows, :] += dot_nt(prob.astype(BF16), do_t[heads, cols])
 
-    def backward_block(h, i, keep):
+    def backward_block(h, i, lo, size, keep):
         heads = slice(h * HD, (h + 1) * HD) if isinstance(h, int) else at(h * HD, HD)
-        cols = slice(i * BLK, (i + 1) * BLK)
+        cols = slice(i * BLK + lo, i * BLK + lo + size)
         doi = do_t[heads, cols]
         delta = jnp.sum(doi.astype(F32) * o_t[heads, cols].astype(F32), axis=0, keepdims=True)
-        dqi = jnp.zeros((HD, BLK), F32)
+        inv = p_inv[h, :, cols]
+        dqi = jnp.zeros((HD, size), F32)
         for j in range(i + 1):
             rows = slice(j * BLK, (j + 1) * BLK)
-            prob = p_t[h, rows, cols]
+            prob = p_t[h, rows, cols] * inv
             ds = (prob * (dot_nn(v[rows, :], doi) - delta)).astype(BF16)
             dqi += dot_nn(k_t[:, rows], ds)
             if keep:
-                ds_t[h, rows, (i % 2) * BLK:(i % 2 + 1) * BLK] = ds
+                ds_t[h, rows, (i % 2) * BLK + lo:(i % 2) * BLK + lo + size] = ds
             else:
                 add_dkv(h, i, j, prob, ds)
         dq[h, cols, :] = (dqi * SCALE).astype(BF16).T
@@ -266,16 +284,59 @@
         part = dot_nt(wo[:, at(c * CH, CH)], dyb[c, at(far, 2 * BLK), :])
         if j == 0:
             do_acc[...] = part
-        elif j < NCH - 1:
+        else:
             do_acc[...] += part
-        else:
-            do_t[:, at(far, 2 * BLK)] = (do_acc[...] + part).astype(BF16)
-        if j < NCH // 2:
-            dwo_send[j] = dot_nn(o_t[...], dyb[c]).astype(BF16)
-            send(f'dwo{j}', dwo_send.at[j], dwo_recv.at[j], peer, 'dwo')
-
+        dwo_send[j] = dot_nn(o_t[...], dyb[c]).astype(BF16)
+        send('dwo', dwo_send.at[j], dwo_recv.at[j], peer)
+
+    def forward_group(g):
+        block = dyb.at[late, group_row(partner_row, g)]
+        arrived(f'dy_late{g}', block, partner)
+        send(f'dy_lfwd{g}', block, block, mate, 'dy_lfwd')
+
+    def finish_do(row, g):
+        with jax.named_scope('do_late'):
+            cols = group_row(row, g)
+            acc = do_acc[:, group_row(row - far, g)]
+            for j in range(NCH // 2):
+                c = data * (NCH // 2) + j
+                acc += dot_nt(wo[:, at(c * CH, CH)], dyb[c, cols, :])
+            do_t[:, cols] = acc.astype(BF16)
+
+    def backward_far(g):
+        def block_of(diag):
+            for c in range(2):
+                for n in range(2):
+                    @pl.when((chip == c) & (core == n))
+                    def _(c=c, n=n):
+                        with jax.named_scope('bwd_far'):
+                            for h in range(HEADS):
+                                backward_block(h, 2 * (1 - c) + (1 - n if diag else n), g * GRP, GRP, True)
+        finish_do(partner_row, g)
+        arrived(f'dy_lfwd{g}', dyb.at[late, group_row(diag_row, g)], mate)
+        finish_do(diag_row, g)
+        block_of(True)
+        send(f'dq_far{g}', dq.at[:, group_row(diag_row, g)], dq_mate.at[1 - chip, :, g * GRP:(g + 1) * GRP], mate, 'dq')
+        block_of(False)
+        arrived(f'dq_far{g}', dq_mate.at[1 - chip, :, g * GRP:(g + 1) * GRP], mate)
+
+    def dx_cols(block, lo, size, cols):
+        rows = at((block * 2 + core) * BLK + lo, size, GRP)
+        acc = jnp.zeros((size, cols.stop - cols.start), F32)
+        for h in range(HEADS):
+            acc += dot_nt(dq[h, rows, :], wq4[core * HEADS + h, cols, :])
+            acc += dot_nt(dq_mate[block, h, lo:lo + size], wq4[(1 - core) * HEADS + h, cols, :])
+        return acc
+
+    def send_dx(g):
+        with jax.named_scope('dx'):
+            for j in range(NDX):
+                n = g * NDX + j
+                dx_send[n] = dx_cols(1 - chip, g * GRP, GRP, slice(j * DXC, (j + 1) * DXC)).astype(BF16)
+                send(f'dx{max(n, NDX)}' if g else 'dx', dx_send.at[n], dx_recv.at[n], partner, 'dx')
+
+    take_chunk(0)
     forward_dy(1)
-    take_chunk(0)
     forward_dy(2)
     take_chunk(1)
     take_chunk(2)
@@ -286,65 +347,19 @@
         def _(c=c):
             def step(h):
                 for i in (2 * c, 2 * c + 1):
-                    backward_block(h, i, False)
+                    backward_block(h, i, 0, BLK, False)
             with jax.named_scope('bwd_near'):
                 over_heads(step)
     send('dq_near', dq.at[:, at(mate_row, BLK)], dq_mate.at[chip], mate, 'dq')
-    forward_dy(4)
     take_chunk(3)
-    forward_dy(5)
-    take_chunk(4)
-    take_chunk(5)
     with jax.named_scope('flip2'):
         flip_x(far)
-    for j in range(6, NCH):
-        forward_dy(j)
-        take_chunk(j)
-
-    for c in range(2):
-        for first in range(2):
-            @pl.when((chip == c) & (core == 1 - first))
-            def _(c=c, first=first):
-                with jax.named_scope('bwd_far0'):
-                    for h in range(HEADS):
-                        backward_block(h, 2 * (1 - c) + first, True)
-    send('dq_far', dq.at[:, at(diag_row, BLK)], dq_mate.at[1 - chip], mate, 'dq')
-    for c in range(2):
-        for first in range(2):
-            @pl.when((chip == c) & (core == 1 - first))
-            def _(c=c, first=first):
-                with jax.named_scope('bwd_far1'):
-                    for h in range(HEADS):
-                        backward_block(h, 2 * (1 - c) + 1 - first, True)
     arrived('wq_mate', wq4.at[pl.ds((1 - core) * HEADS, HEADS)], mate)
-    arrived('dq_far', dq_mate.at[1 - chip], mate)
-
-    def dx_cols(block, cols):
-        rows = at((block * 2 + core) * BLK, BLK)
-        acc = jnp.zeros((BLK, DXC), F32)
-        for h in range(HEADS):
-            acc += dot_nt(dq[h, rows, :], wq4[core * HEADS + h, cols, :])
-            acc += dot_nt(dq_mate[block, h], wq4[(1 - core) * HEADS + h, cols, :])
-        return acc
-
-    def send_dx(j):
-        dx_send[j] = dx_cols(1 - chip, slice(j * DXC, (j + 1) * DXC)).astype(BF16)
-        send(f'dx{j}', dx_send.at[j], dx_recv.at[j], partner, 'dx')
-
+    forward_group(0)
+    backward_far(0)
     send_dx(0)
-    send_dx(1)
-    for c in range(2):
-        @pl.when(chip == c)
-        def _(c=c):
-            def step(h):
-                for i in (2 * (1 - c), 2 * (1 - c) + 1):
-                    for j in range(i + 1):
-                        rows = slice(j * BLK, (j + 1) * BLK)
-                        add_dkv(h, i, j, p_t[h, rows, i * BLK:(i + 1) * BLK],
-                                ds_t[h, rows, (i % 2) * BLK:(i % 2 + 1) * BLK])
-            with jax.named_scope('dkv'):
-                over_heads(step)
-    send('dkv_mate', dkv.at[1 - core], dkv_mate, mate)
+    forward_group(1)
+    backward_far(1)
 
     def send_dwq(r):
         with jax.named_scope('dwq'):
@@ -353,22 +368,36 @@
                 dwq_send[r, h] = dot_nn(x_t[rows, :], dq[h]).astype(BF16)
             send(f'dwq{r}', dwq_send.at[r], dwq_recv.at[r], peer, 'dwq')
     send_dwq(0)
+    for c in range(2):
+        @pl.when(chip == c)
+        def _(c=c):
+            def step(h):
+                for i in (2 * (1 - c), 2 * (1 - c) + 1):
+                    cols = slice(i * BLK, (i + 1) * BLK)
+                    for j in range(i + 1):
+                        rows = slice(j * BLK, (j + 1) * BLK)
+                        add_dkv(h, i, j, p_t[h, rows, cols] * p_inv[h, :, cols],
+                                ds_t[h, rows, (i % 2) * BLK:(i % 2 + 1) * BLK])
+            with jax.named_scope('dkv'):
+                over_heads(step)
+    send('dkv_mate', dkv.at[1 - core], dkv_mate, mate)
+
+    for r in range(1, 4):
+        send_dwq(r)
     arrived('dkv_mate', dkv_mate, mate)
     factor = jnp.where(core == 0, SCALE, 1.0).astype(F32)
     summed = (dkv[core] + dkv_mate[...]) * factor
     dkv_mate[...] = summed
     dkv_send[...] = summed.astype(BF16)
     send('dkv_far', dkv_send, dkv_part, partner)
-    send_dx(2)
-    send_dx(3)
-    for r in range(1, 4):
-        send_dwq(r)
+    send_dx(1)
 
     arrived('dq_near', dq_mate.at[chip], mate)
-    for j in range(NDX):
-        dx_own[:, j * DXC:(j + 1) * DXC] = dx_cols(chip, slice(j * DXC, (j + 1) * DXC))
+    for j in range(4):
+        cols = slice(j * 512, (j + 1) * 512)
+        dx_own[:, cols] = dx_cols(chip, 0, BLK, cols)
+    arrived('dwo', dwo_recv, peer)
     for j in range(NCH // 2):
-        arrived(f'dwo{j}', dwo_recv.at[j], peer)
         cols = slice(j * CH, (j + 1) * CH)
         dwo_out[:, cols] = dot_nn(o_t[...], dyb[chunk_at(NCH // 2 + j)]) + dwo_recv[j].astype(F32)
 
@@ -383,18 +412,19 @@
     kept_rows = at((model * 2 + data) * 256, 256)
     dwk_out[...] = dot_nn(x_t[kept_rows, :], dkv_full[0])
     dwv_out[...] = dot_nn(x_t[kept_rows, :], dkv_full[1])
-    for j in range(NDX):
-        cols = slice(j * DXC, (j + 1) * DXC)
+    for j in range(4):
+        cols = slice(j * 512, (j + 1) * 512)
         dx_own[:, cols] += (dot_nt(dkv_full[0, at(own_row, BLK), :], wkv[0, cols, :])
                             + dot_nt(dkv_full[1, at(own_row, BLK), :], wkv[1, cols, :]))
 
-    def finish_dx(j):
-        arrived(f'dx{j}', dx_recv.at[j], partner)
-        cols = slice(j * DXC, (j + 1) * DXC)
-        dx_out[:, cols] = (dx_own[:, cols] + dx_recv[j].astype(F32)).astype(BF16)
-
-    finish_dx(0)
-    finish_dx(1)
+    def finish_dx(n):
+        rows = slice(n // NDX * GRP, (n // NDX + 1) * GRP)
+        cols = slice(n % NDX * DXC, (n % NDX + 1) * DXC)
+        dx_out[rows, cols] = (dx_own[rows, cols] + dx_recv[n].astype(F32)).astype(BF16)
+
+    arrived('dx', dx_recv.at[:NDX], partner)
+    for n in range(NDX):
+        finish_dx(n)
     for r in range(4):
         arrived(f'dwq{r}', dwq_recv.at[r], peer)
         with jax.named_scope('dwq_sum'):
@@ -402,11 +432,12 @@
             for h in range(HEADS):
                 value = dot_nn(x_t[rows, :], dq[h]) + dwq_recv[r, h].astype(F32)
                 dwq_out[r * 256:(r + 1) * 256, h, :] = value
-    finish_dx(2)
+    for n in range(NDX, 2 * NDX):
+        arrived(f'dx{n}', dx_recv.at[n], partner)
+        finish_dx(n)
     arrived('dwkv', dwkv_recv, peer)
     dwk_out[...] += dwkv_recv[0].astype(F32)
     dwv_out[...] += dwkv_recv[1].astype(F32)
-    finish_dx(3)
     with jax.named_scope('sends'):
         sent('x_far', x_ref)
         sent('x_mate', x_ref)
@@ -414,7 +445,8 @@
         sent('dy_mate', dy_ref)
         sent('wq_mate', wq4.at[pl.ds(core * HEADS, HEADS)])
         sent('x_fwd', xb.at[at(partner_row, BLK)])
-        sent('dy_fwd', dyb.at[:, at(partner_row, BLK)])
+        sent('dy_fwd', dyb.at[late, at(partner_row, BLK)])
+        sent('dy_lfwd', dyb.at[late, at(partner_row, BLK)])
         sent('dwo', dwo_send)
         sent('dq', dq_mate)
         sent('dx', dx_send)
@@ -443,6 +475,7 @@
         pltpu.VMEM((HD, SEQ), BF16),
         pltpu.VMEM((HD, SEQ), BF16),
         pltpu.VMEM((HEADS, SEQ, SEQ), F32),
+        pltpu.VMEM((HEADS, 1, SEQ), F32),
         pltpu.VMEM((HEADS, SEQ, 2 * BLK), BF16),
         pltpu.VMEM((HEADS * HD, SEQ), BF16),
         pltpu.VMEM((HEADS * HD, 2 * BLK), F32),
@@ -459,12 +492,12 @@
         pltpu.VMEM((4, HEADS, HALF // 4, HD), BF16),
         pltpu.VMEM((4, HEADS, HALF // 4, HD), BF16),
         pltpu.VMEM((BLK, DIM), F32),
-        pltpu.VMEM((NDX, BLK, DXC), BF16),
-        pltpu.VMEM((NDX, BLK, DXC), BF16),
+        pltpu.VMEM((2 * NDX, GRP, DXC), BF16),
+        pltpu.VMEM((2 * NDX, GRP, DXC), BF16),
         pltpu.VMEM((2, 256, HD), BF16),
         pltpu.VMEM((2, 256, HD), BF16),
-        pltpu.SemaphoreType.DMA((15,)),
-        pltpu.SemaphoreType.DMA((43,)),
+        pltpu.SemaphoreType.DMA((16,)),
+        pltpu.SemaphoreType.DMA((39,)),
         pltpu.SemaphoreType.DMA((6,)),
     ]
     return pl.pallas_call(

time: 93.5 us -> 91.3 us (0.976)
  Pallas kernels: 92.6 us -> 90.4 us
    pallas_call x1, Pallas kernels: 90 us -> 87.8 us  [fused_step(): pl.pallas_call(body, out_shape=(pltpu.VMEM((BLK, DIM), BF16), pltpu.VMEM(...]
where the time goes in v4:
time: 91.3 us; the launch traced here: 91.2 us
  Pallas kernels  90.4 us (99%)
    pallas_call x1, Pallas kernels, fused_step(): pl.pallas_call(body, out_shape=(pltpu.VMEM((BLK, DIM), BF16), pltpu.VMEM(...  87.8 us
    pallas_call x1, Pallas kernels, flush(): pl.pallas_call(flush_body, out_shape=tuple((jax.ShapeDtypeStruct(a.shape,...  2.57 us

profile of v4, /device:TPU:0, one launch (start us, length us, event | category | flops | bytes accessed | tf_op | source)
XLA Modules:
  0.0 91.2 jit_solution(2527323123093228406)
XLA Ops:
  0.6 87.8 %attention_backward.1 = (bf16[256,2048]{1,0:T(8,128)(2,1)S(1)}, f32[1024,2,256]{2,1,0:T(2,128)S(1)}, f32[256,256]{1,0:T(8,128)S(1)}, f32[256,256]{1,0:T(8,128)S(1)}, f32[512,1024]{1,0:T(8,128)S(1)}) custom-call(bf16[256,2048]{1,0:T(8,128)(2,1)} %bitcast.8, bf16[256,2048]{1,0:T(8,128)(2,1)} %bitcast.9, bf16[2048,2,256]{2,1,0:T(2,128)(2,1)} %wq_ref.1, ...), custom_call_target="tpu_custom_call" | custom-call | tf_op jit(solution)/shard_map/attention_backward/pallas_call | solution.py:503
  88.5 2.6 %write_results.1 = (bf16[256,2048]{1,0:T(8,128)(2,1)}, f32[1024,2,256]{2,1,0:T(2,128)}, f32[256,256]{1,0:T(8,128)}, f32[256,256]{1,0:T(8,128)}, f32[512,1024]{1,0:T(8,128)}) custom-call(bf16[256,2048]{1,0:T(8,128)(2,1)S(1)} %get-tuple-element.15.refs_0_, f32[1024,2,256]{2,1,0:T(2,128)S(1)} %get-tuple-element.16.refs_1_, ...), custom_call_target="tpu_custom_call" | custom-call | tf_op jit(solution)/shard_map/write_results/pallas_call | solution.py:530

commit v5 on v4

--- a/solution.py
+++ b/solution.py
@@ -100,10 +100,13 @@
         return at(row + g * GRP, GRP, GRP)
 
     def send_dy():
-        for j in range(NCH // 2):
+        for j in range(NCH // 2 - 1):
             c = chunk_at(j)
             send(f'dy_far{j}', dy_ref.at[:, at(c * CH, CH)], dyb.at[c, at(own_row, BLK)], partner, 'dy_far')
         for g in range(2):
+            c = chunk_at(NCH // 2 - 1)
+            send(f'dy_split{g}', dy_ref.at[g * GRP:(g + 1) * GRP, at(c * CH, CH)],
+                 dyb.at[c, group_row(own_row, g)], partner, 'dy_far')
             for j in range(NCH // 2):
                 c = data * (NCH // 2) + j
                 send(f'dy_late{g}', dy_ref.at[g * GRP:(g + 1) * GRP, at(c * CH, CH)],
@@ -224,7 +227,7 @@
 
     mask = lax.broadcasted_iota(jnp.int32, (BLK, BLK), 0) <= lax.broadcasted_iota(jnp.int32, (BLK, BLK), 1)
 
-    def forward_block(h, i):
+    def scores(h, i):
         heads = slice(h * HD, (h + 1) * HD)
         cols = slice(i * BLK, (i + 1) * BLK)
         rows = (i + 1) * BLK
@@ -235,17 +238,31 @@
         top = jnp.max(p_t[h, :rows, cols], axis=0, keepdims=True)
         e = jnp.exp(p_t[h, :rows, cols] - top)
         p_t[h, :rows, cols] = e
-        inv = 1.0 / jnp.sum(e, axis=0, keepdims=True)
-        p_inv[h, :, cols] = inv
-        prob = (p_t[h, :rows, cols] * inv).astype(BF16)
-        o_t[heads, cols] = dot_nn(v_t[:, :rows], prob).astype(BF16)
+        p_inv[h, :, cols] = 1.0 / jnp.sum(e, axis=0, keepdims=True)
+
+    def values(h, i):
+        cols = slice(i * BLK, (i + 1) * BLK)
+        rows = (i + 1) * BLK
+        prob = (p_t[h, :rows, cols] * p_inv[h, :, cols]).astype(BF16)
+        o_t[h * HD:(h + 1) * HD, cols] = dot_nn(v_t[:, :rows], prob).astype(BF16)
+
+    def on_core(n, step):
+        @pl.when(core == n)
+        def _():
+            step()
+
     with jax.named_scope('fwd'):
-        for i in range(3):
+        for i in range(2):
             for h in range(HEADS):
-                forward_block(h, i)
-        forward_dy(0)
-        for h in range(HEADS):
-            forward_block(h, 3)
+                scores(h, i)
+        on_core(1, lambda: forward_dy(0))
+        for i in range(2, 4):
+            for h in range(HEADS):
+                scores(h, i)
+        on_core(0, lambda: forward_dy(0))
+        for i in range(4):
+            for h in range(HEADS):
+                values(h, i)
 
     def add_dkv(h, i, j, prob, ds):
         rows = slice(j * BLK, (j + 1) * BLK)
@@ -281,27 +298,41 @@
     def take_chunk(j):
         c = chunk_at(j)
         arrived(f'dy_fwd{j}', dyb.at[c, at(diag_row, BLK)], mate)
+        dwo_send[j] = dot_nn(o_t[...], dyb[c]).astype(BF16)
+        send('dwo', dwo_send.at[j], dwo_recv.at[j], peer)
         part = dot_nt(wo[:, at(c * CH, CH)], dyb[c, at(far, 2 * BLK), :])
         if j == 0:
             do_acc[...] = part
         else:
             do_acc[...] += part
-        dwo_send[j] = dot_nn(o_t[...], dyb[c]).astype(BF16)
-        send('dwo', dwo_send.at[j], dwo_recv.at[j], peer)
+
+    split = chunk_at(NCH // 2 - 1)
+
+    def forward_split(g):
+        block = dyb.at[split, group_row(partner_row, g)]
+        arrived(f'dy_split{g}', block, partner)
+        send(f'dy_sfwd{g}', block, block, mate, 'dy_fwd')
+
+    def take_split():
+        arrived('dy_sfwd1', dyb.at[split, group_row(diag_row, 1)], mate)
+        with jax.named_scope('dwo3'):
+            dwo_send[NCH // 2 - 1] = dot_nn(o_t[...], dyb[split]).astype(BF16)
+            send('dwo', dwo_send.at[NCH // 2 - 1], dwo_recv.at[NCH // 2 - 1], peer)
 
     def forward_group(g):
         block = dyb.at[late, group_row(partner_row, g)]
         arrived(f'dy_late{g}', block, partner)
         send(f'dy_lfwd{g}', block, block, mate, 'dy_lfwd')
 
-    def finish_do(row, g):
+    def finish_do(rows, g):
         with jax.named_scope('do_late'):
-            cols = group_row(row, g)
-            acc = do_acc[:, group_row(row - far, g)]
-            for j in range(NCH // 2):
-                c = data * (NCH // 2) + j
-                acc += dot_nt(wo[:, at(c * CH, CH)], dyb[c, cols, :])
-            do_t[:, cols] = acc.astype(BF16)
+            cols = [group_row(row, g) for row in rows]
+            accs = [do_acc[:, group_row(row - far, g)] for row in rows]
+            for c in [split] + [data * (NCH // 2) + j for j in range(NCH // 2)]:
+                part = dot_nt(wo[:, at(c * CH, CH)], jnp.concatenate([dyb[c, n, :] for n in cols], axis=0))
+                accs = [acc + part[:, n * GRP:(n + 1) * GRP] for n, acc in enumerate(accs)]
+            for n, acc in zip(cols, accs):
+                do_t[:, n] = acc.astype(BF16)
 
     def backward_far(g):
         def block_of(diag):
@@ -312,11 +343,16 @@
                         with jax.named_scope('bwd_far'):
                             for h in range(HEADS):
                                 backward_block(h, 2 * (1 - c) + (1 - n if diag else n), g * GRP, GRP, True)
-        finish_do(partner_row, g)
+        if g == 0:
+            finish_do([partner_row], g)
+            forward_split(1)
+            arrived('dy_sfwd0', dyb.at[split, group_row(diag_row, 0)], mate)
         arrived(f'dy_lfwd{g}', dyb.at[late, group_row(diag_row, g)], mate)
-        finish_do(diag_row, g)
+        finish_do([diag_row] if g == 0 else [partner_row, diag_row], g)
         block_of(True)
         send(f'dq_far{g}', dq.at[:, group_row(diag_row, g)], dq_mate.at[1 - chip, :, g * GRP:(g + 1) * GRP], mate, 'dq')
+        if g == 0:
+            take_split()
         block_of(False)
         arrived(f'dq_far{g}', dq_mate.at[1 - chip, :, g * GRP:(g + 1) * GRP], mate)
 
@@ -328,9 +364,9 @@
             acc += dot_nt(dq_mate[block, h, lo:lo + size], wq4[(1 - core) * HEADS + h, cols, :])
         return acc
 
-    def send_dx(g):
+    def send_dx(g, pieces):
         with jax.named_scope('dx'):
-            for j in range(NDX):
+            for j in pieces:
                 n = g * NDX + j
                 dx_send[n] = dx_cols(1 - chip, g * GRP, GRP, slice(j * DXC, (j + 1) * DXC)).astype(BF16)
                 send(f'dx{max(n, NDX)}' if g else 'dx', dx_send.at[n], dx_recv.at[n], partner, 'dx')
@@ -340,7 +376,6 @@
     forward_dy(2)
     take_chunk(1)
     take_chunk(2)
-    forward_dy(3)
 
     for c in range(2):
         @pl.when(chip == c)
@@ -351,14 +386,15 @@
             with jax.named_scope('bwd_near'):
                 over_heads(step)
     send('dq_near', dq.at[:, at(mate_row, BLK)], dq_mate.at[chip], mate, 'dq')
-    take_chunk(3)
     with jax.named_scope('flip2'):
         flip_x(far)
     arrived('wq_mate', wq4.at[pl.ds((1 - core) * HEADS, HEADS)], mate)
+    forward_split(0)
     forward_group(0)
     backward_far(0)
-    send_dx(0)
+    send_dx(0, (0, 1))
     forward_group(1)
+    send_dx(0, (2, 3))
     backward_far(1)
 
     def send_dwq(r):
@@ -390,7 +426,7 @@
     dkv_mate[...] = summed
     dkv_send[...] = summed.astype(BF16)
     send('dkv_far', dkv_send, dkv_part, partner)
-    send_dx(1)
+    send_dx(1, range(NDX))
 
     arrived('dq_near', dq_mate.at[chip], mate)
     for j in range(4):
@@ -497,7 +533,7 @@
         pltpu.VMEM((2, 256, HD), BF16),
         pltpu.VMEM((2, 256, HD), BF16),
         pltpu.SemaphoreType.DMA((16,)),
-        pltpu.SemaphoreType.DMA((39,)),
+        pltpu.SemaphoreType.DMA((41,)),
         pltpu.SemaphoreType.DMA((6,)),
     ]
     return pl.pallas_call(

time: 91.3 us -> 90.2 us (0.988)
  Pallas kernels: 90.4 us -> 89.3 us
    pallas_call x1, Pallas kernels: 87.8 us -> 86.8 us  [fused_step(): pl.pallas_call(body, out_shape=(pltpu.VMEM((BLK, DIM), BF16), pltpu.VMEM(...]
where the time goes in v5:
time: 90.2 us
  Pallas kernels  89.3 us (99%)
    pallas_call x1, Pallas kernels, fused_step(): pl.pallas_call(body, out_shape=(pltpu.VMEM((BLK, DIM), BF16), pltpu.VMEM(...  86.8 us
    pallas_call x1, Pallas kernels, flush(): pl.pallas_call(flush_body, out_shape=tuple((jax.ShapeDtypeStruct(a.shape,...  2.57 us

profile of v5, /device:TPU:0, one launch (start us, length us, event | category | flops | bytes accessed | tf_op | source)
XLA Modules:
  0.0 90.2 jit_solution(3116875237458919848)
XLA Ops:
  0.6 86.8 %attention_backward.1 = (bf16[256,2048]{1,0:T(8,128)(2,1)S(1)}, f32[1024,2,256]{2,1,0:T(2,128)S(1)}, f32[256,256]{1,0:T(8,128)S(1)}, f32[256,256]{1,0:T(8,128)S(1)}, f32[512,1024]{1,0:T(8,128)S(1)}) custom-call(bf16[256,2048]{1,0:T(8,128)(2,1)} %bitcast.8, bf16[256,2048]{1,0:T(8,128)(2,1)} %bitcast.9, bf16[2048,2,256]{2,1,0:T(2,128)(2,1)} %wq_ref.1, ...), custom_call_target="tpu_custom_call" | custom-call | tf_op jit(solution)/shard_map/attention_backward/pallas_call | solution.py:539
  87.4 2.6 %write_results.1 = (bf16[256,2048]{1,0:T(8,128)(2,1)}, f32[1024,2,256]{2,1,0:T(2,128)}, f32[256,256]{1,0:T(8,128)}, f32[256,256]{1,0:T(8,128)}, f32[512,1024]{1,0:T(8,128)}) custom-call(bf16[256,2048]{1,0:T(8,128)(2,1)S(1)} %get-tuple-element.15.refs_0_, f32[1024,2,256]{2,1,0:T(2,128)S(1)} %get-tuple-element.16.refs_1_, ...), custom_call_target="tpu_custom_call" | custom-call | tf_op jit(solution)/shard_map/write_results/pallas_call | solution.py:566

commit v6 on v5

--- a/solution.py
+++ b/solution.py
@@ -334,26 +334,20 @@
             for n, acc in zip(cols, accs):
                 do_t[:, n] = acc.astype(BF16)
 
-    def backward_far(g):
-        def block_of(diag):
-            for c in range(2):
-                for n in range(2):
-                    @pl.when((chip == c) & (core == n))
-                    def _(c=c, n=n):
-                        with jax.named_scope('bwd_far'):
-                            for h in range(HEADS):
-                                backward_block(h, 2 * (1 - c) + (1 - n if diag else n), g * GRP, GRP, True)
-        if g == 0:
-            finish_do([partner_row], g)
-            forward_split(1)
-            arrived('dy_sfwd0', dyb.at[split, group_row(diag_row, 0)], mate)
-        arrived(f'dy_lfwd{g}', dyb.at[late, group_row(diag_row, g)], mate)
-        finish_do([diag_row] if g == 0 else [partner_row, diag_row], g)
-        block_of(True)
+    def far_blocks(g, heads, blocks_of):
+        for c in range(2):
+            for n in range(2):
+                @pl.when((chip == c) & (core == n))
+                def _(c=c, n=n):
+                    with jax.named_scope('bwd_far'):
+                        for h in heads:
+                            for b in blocks_of(n):
+                                backward_block(h, 2 * (1 - c) + b, g * GRP, GRP, True)
+
+    def exchange_dq(g):
         send(f'dq_far{g}', dq.at[:, group_row(diag_row, g)], dq_mate.at[1 - chip, :, g * GRP:(g + 1) * GRP], mate, 'dq')
-        if g == 0:
-            take_split()
-        block_of(False)
+
+    def arrived_dq(g):
         arrived(f'dq_far{g}', dq_mate.at[1 - chip, :, g * GRP:(g + 1) * GRP], mate)
 
     def dx_cols(block, lo, size, cols):
@@ -389,21 +383,40 @@
     with jax.named_scope('flip2'):
         flip_x(far)
     arrived('wq_mate', wq4.at[pl.ds((1 - core) * HEADS, HEADS)], mate)
+    def send_dwq(r, heads):
+        with jax.named_scope('dwq'):
+            rows = at((1 - data) * HALF + r * 256, 256)
+            for h in heads:
+                dwq_send[r, h] = dot_nn(x_t[rows, :], dq[h]).astype(BF16)
+                send(f'dwq{r}', dwq_send.at[r, h], dwq_recv.at[r, h], peer, 'dwq')
+
     forward_split(0)
     forward_group(0)
-    backward_far(0)
+    finish_do([partner_row], 0)
+    far_blocks(0, range(HEADS), lambda n: (n,))
+    forward_split(1)
+    arrived('dy_sfwd0', dyb.at[split, group_row(diag_row, 0)], mate)
+    arrived('dy_lfwd0', dyb.at[late, group_row(diag_row, 0)], mate)
+    finish_do([diag_row], 0)
+    far_blocks(0, range(HEADS), lambda n: (1 - n,))
+    exchange_dq(0)
+    take_split()
+    arrived_dq(0)
     send_dx(0, (0, 1))
     forward_group(1)
     send_dx(0, (2, 3))
-    backward_far(1)
-
-    def send_dwq(r):
-        with jax.named_scope('dwq'):
-            rows = at((1 - data) * HALF + r * 256, 256)
-            for h in range(HEADS):
-                dwq_send[r, h] = dot_nn(x_t[rows, :], dq[h]).astype(BF16)
-            send(f'dwq{r}', dwq_send.at[r], dwq_recv.at[r], peer, 'dwq')
-    send_dwq(0)
+    arrived('dy_lfwd1', dyb.at[late, group_row(diag_row, 1)], mate)
+    finish_do([partner_row, diag_row], 1)
+    for h in range(HEADS):
+        for c in range(2):
+            @pl.when(chip == c)
+            def _(c=c):
+                with jax.named_scope('bwd_far'):
+                    for b in range(2):
+                        backward_block(h, 2 * (1 - c) + b, GRP, GRP, True)
+        for r in range(2):
+            send_dwq(r, [h])
+    exchange_dq(1)
     for c in range(2):
         @pl.when(chip == c)
         def _(c=c):
@@ -418,8 +431,9 @@
                 over_heads(step)
     send('dkv_mate', dkv.at[1 - core], dkv_mate, mate)
 
-    for r in range(1, 4):
-        send_dwq(r)
+    for r in range(2, 4):
+        send_dwq(r, range(HEADS))
+    arrived_dq(1)
     arrived('dkv_mate', dkv_mate, mate)
     factor = jnp.where(core == 0, SCALE, 1.0).astype(F32)
     summed = (dkv[core] + dkv_mate[...]) * factor

time: 90.2 us -> 89.4 us (level)
  no operation moved by 1% of the time
where the time goes in v6:
time: 89.4 us; the launch traced here: 89.3 us
  Pallas kernels  88.5 us (99%)
    pallas_call x1, Pallas kernels, fused_step(): pl.pallas_call(body, out_shape=(pltpu.VMEM((BLK, DIM), BF16), pltpu.VMEM(...  85.9 us
    pallas_call x1, Pallas kernels, flush(): pl.pallas_call(flush_body, out_shape=tuple((jax.ShapeDtypeStruct(a.shape,...  2.57 us

profile of v6, /device:TPU:0, one launch (start us, length us, event | category | flops | bytes accessed | tf_op | source)
XLA Modules:
  0.0 89.3 jit_solution(13590781544672329906)
XLA Ops:
  0.6 85.9 %attention_backward.1 = (bf16[256,2048]{1,0:T(8,128)(2,1)S(1)}, f32[1024,2,256]{2,1,0:T(2,128)S(1)}, f32[256,256]{1,0:T(8,128)S(1)}, f32[256,256]{1,0:T(8,128)S(1)}, f32[512,1024]{1,0:T(8,128)S(1)}) custom-call(bf16[256,2048]{1,0:T(8,128)(2,1)} %bitcast.8, bf16[256,2048]{1,0:T(8,128)(2,1)} %bitcast.9, bf16[2048,2,256]{2,1,0:T(2,128)(2,1)} %wq_ref.1, ...), custom_call_target="tpu_custom_call" | custom-call | tf_op jit(solution)/shard_map/attention_backward/pallas_call | solution.py:553
  86.5 2.6 %write_results.1 = (bf16[256,2048]{1,0:T(8,128)(2,1)}, f32[1024,2,256]{2,1,0:T(2,128)}, f32[256,256]{1,0:T(8,128)}, f32[256,256]{1,0:T(8,128)}, f32[512,1024]{1,0:T(8,128)}) custom-call(bf16[256,2048]{1,0:T(8,128)(2,1)S(1)} %get-tuple-element.15.refs_0_, f32[1024,2,256]{2,1,0:T(2,128)S(1)} %get-tuple-element.16.refs_1_, ...), custom_call_target="tpu_custom_call" | custom-call | tf_op jit(solution)/shard_map/write_results/pallas_call | solution.py:580

commit v7 on v6

--- a/solution.py
+++ b/solution.py
@@ -19,6 +19,10 @@
 DXC = 512
 NDX = DIM // DXC
 GRP = 128
+SHARED = {**dict.fromkeys(('x_far', 'x_mate', 'dy_far', 'dy_mate'), 'inputs'),
+          **dict.fromkeys(('x_fwd', 'dwo', 'dwq', 'dx'), 'mib'),
+          **dict.fromkeys(('wq_mate', 'dy_fwd', 'dy_lfwd', 'dkv_mate'), 'pair'),
+          **dict.fromkeys(('dkv_far', 'dkv_full'), 'dkv'), 'dq': 'dq', 'dwkv': 'dwkv'}
 PIECE = 64
 NP = BLK // PIECE
 HALF = DIM // 2
@@ -64,7 +68,7 @@
     devices = {}
 
     def send(name, src, dst, device, group=None, part=None):
-        group = group or name
+        group = SHARED[group or name]
         devices[group] = device
         copy = pltpu.make_async_remote_copy(
             src_ref=src, dst_ref=dst, send_sem=sems.at[groups.setdefault(group, len(groups))],
@@ -298,8 +302,10 @@
     def take_chunk(j):
         c = chunk_at(j)
         arrived(f'dy_fwd{j}', dyb.at[c, at(diag_row, BLK)], mate)
-        dwo_send[j] = dot_nn(o_t[...], dyb[c]).astype(BF16)
-        send('dwo', dwo_send.at[j], dwo_recv.at[j], peer)
+        for h in range(HEADS):
+            heads = slice(h * HD, (h + 1) * HD)
+            dwo_send[j, heads, :] = dot_nn(o_t[heads, :], dyb[c]).astype(BF16)
+            send('dwo', dwo_send.at[j, heads], dwo_recv.at[j, heads], peer)
         part = dot_nt(wo[:, at(c * CH, CH)], dyb[c, at(far, 2 * BLK), :])
         if j == 0:
             do_acc[...] = part
@@ -363,7 +369,7 @@
             for j in pieces:
                 n = g * NDX + j
                 dx_send[n] = dx_cols(1 - chip, g * GRP, GRP, slice(j * DXC, (j + 1) * DXC)).astype(BF16)
-                send(f'dx{max(n, NDX)}' if g else 'dx', dx_send.at[n], dx_recv.at[n], partner, 'dx')
+                send(f'dx{max(n, NDX + 1)}' if g else 'dx', dx_send.at[n], dx_recv.at[n], partner, 'dx')
 
     take_chunk(0)
     forward_dy(1)
@@ -388,7 +394,7 @@
             rows = at((1 - data) * HALF + r * 256, 256)
             for h in heads:
                 dwq_send[r, h] = dot_nn(x_t[rows, :], dq[h]).astype(BF16)
-                send(f'dwq{r}', dwq_send.at[r, h], dwq_recv.at[r, h], peer, 'dwq')
+                send('dwq' if r < 3 else 'dwq3', dwq_send.at[r, h], dwq_recv.at[r, h], peer, 'dwq')
 
     forward_split(0)
     forward_group(0)
@@ -475,35 +481,28 @@
     arrived('dx', dx_recv.at[:NDX], partner)
     for n in range(NDX):
         finish_dx(n)
+    arrived('dwq', dwq_recv.at[:3], peer)
     for r in range(4):
-        arrived(f'dwq{r}', dwq_recv.at[r], peer)
+        if r == 3:
+            arrived('dwq3', dwq_recv.at[3], peer)
         with jax.named_scope('dwq_sum'):
             rows = at(data * HALF + r * 256, 256)
             for h in range(HEADS):
                 value = dot_nn(x_t[rows, :], dq[h]) + dwq_recv[r, h].astype(F32)
                 dwq_out[r * 256:(r + 1) * 256, h, :] = value
+    arrived(f'dx{NDX + 1}', dx_recv.at[NDX:NDX + 2], partner)
     for n in range(NDX, 2 * NDX):
-        arrived(f'dx{n}', dx_recv.at[n], partner)
+        if n > NDX + 1:
+            arrived(f'dx{n}', dx_recv.at[n], partner)
         finish_dx(n)
     arrived('dwkv', dwkv_recv, peer)
     dwk_out[...] += dwkv_recv[0].astype(F32)
     dwv_out[...] += dwkv_recv[1].astype(F32)
     with jax.named_scope('sends'):
-        sent('x_far', x_ref)
-        sent('x_mate', x_ref)
-        sent('dy_far', dy_ref)
-        sent('dy_mate', dy_ref)
-        sent('wq_mate', wq4.at[pl.ds(core * HEADS, HEADS)])
-        sent('x_fwd', xb.at[at(partner_row, BLK)])
-        sent('dy_fwd', dyb.at[late, at(partner_row, BLK)])
-        sent('dy_lfwd', dyb.at[late, at(partner_row, BLK)])
-        sent('dwo', dwo_send)
+        for group in ('inputs', 'mib', 'pair'):
+            sent(group, xb)
+        sent('dkv', dkv_full)
         sent('dq', dq_mate)
-        sent('dx', dx_send)
-        sent('dkv_mate', dkv_mate)
-        sent('dkv_far', dkv_send)
-        sent('dkv_full', dkv_send)
-        sent('dwq', dwq_send)
         sent('dwkv', dwkv_send)
     assert len(groups) == sems.shape[0] and len(slots) == recvs.shape[0]
 
@@ -546,8 +545,8 @@
         pltpu.VMEM((2 * NDX, GRP, DXC), BF16),
         pltpu.VMEM((2, 256, HD), BF16),
         pltpu.VMEM((2, 256, HD), BF16),
-        pltpu.SemaphoreType.DMA((16,)),
-        pltpu.SemaphoreType.DMA((41,)),
+        pltpu.SemaphoreType.DMA((6,)),
+        pltpu.SemaphoreType.DMA((38,)),
         pltpu.SemaphoreType.DMA((6,)),
     ]
     return pl.pallas_call(

time: 89.4 us -> 89 us (level)
  no operation moved by 1% of the time
where the time goes in v7:
time: 89 us; the launch traced here: 88.9 us
  Pallas kernels  88.1 us (99%)
    pallas_call x1, Pallas kernels, fused_step(): pl.pallas_call(body, out_shape=(pltpu.VMEM((BLK, DIM), BF16), pltpu.VMEM(...  85.6 us
    pallas_call x1, Pallas kernels, flush(): pl.pallas_call(flush_body, out_shape=tuple((jax.ShapeDtypeStruct(a.shape,...  2.57 us

profile of v7, /device:TPU:0, one launch (start us, length us, event | category | flops | bytes accessed | tf_op | source)
XLA Modules:
  0.0 88.9 jit_solution(17317291998904185407)
XLA Ops:
  0.6 85.6 %attention_backward.1 = (bf16[256,2048]{1,0:T(8,128)(2,1)S(1)}, f32[1024,2,256]{2,1,0:T(2,128)S(1)}, f32[256,256]{1,0:T(8,128)S(1)}, f32[256,256]{1,0:T(8,128)S(1)}, f32[512,1024]{1,0:T(8,128)S(1)}) custom-call(bf16[256,2048]{1,0:T(8,128)(2,1)} %bitcast.8, bf16[256,2048]{1,0:T(8,128)(2,1)} %bitcast.9, bf16[2048,2,256]{2,1,0:T(2,128)(2,1)} %wq_ref.1, ...), custom_call_target="tpu_custom_call" | custom-call | tf_op jit(solution)/shard_map/attention_backward/pallas_call | solution.py:552
  86.2 2.6 %write_results.1 = (bf16[256,2048]{1,0:T(8,128)(2,1)}, f32[1024,2,256]{2,1,0:T(2,128)}, f32[256,256]{1,0:T(8,128)}, f32[256,256]{1,0:T(8,128)}, f32[512,1024]{1,0:T(8,128)}) custom-call(bf16[256,2048]{1,0:T(8,128)(2,1)S(1)} %get-tuple-element.15.refs_0_, f32[1024,2,256]{2,1,0:T(2,128)S(1)} %get-tuple-element.16.refs_1_, ...), custom_call_target="tpu_custom_call" | custom-call | tf_op jit(solution)/shard_map/write_results/pallas_call | solution.py:579

commit v8 on v7

--- a/solution.py
+++ b/solution.py
@@ -152,11 +152,11 @@
             return carry
         lax.fori_loop(0, DIM // 256, step, 0)
 
-    def flip_kv(first_row):
+    def flip_kv(first_row, pairs):
         for r in range(2):
             rows = at(first_row + r * BLK, BLK)
-            k_t[:, rows] = k[rows, :].T
-            v_t[:, rows] = v[rows, :].T
+            for src, dst in pairs:
+                dst[:, rows] = src[rows, :].T
 
     with jax.named_scope('loads'):
         for copy in loads:
@@ -178,7 +178,7 @@
             project(xb[rows, :], [(rows, BLK, 0)])
             return carry
         lax.fori_loop(0, 2, project_near, 0)
-        flip_kv(near)
+        flip_kv(near, ((k, k_t), (v, v_t)))
 
     def forward_x(p):
         block = xb.at[x_piece(partner_row, p)]
@@ -222,7 +222,7 @@
     def _():
         send_dy()
     project_far(3)
-    flip_kv(far)
+    flip_kv(far, ((v, v_t),))
 
     def forward_dy(j):
         block = dyb.at[chunk_at(j), at(partner_row, BLK)]
@@ -376,6 +376,7 @@
     forward_dy(2)
     take_chunk(1)
     take_chunk(2)
+    flip_kv(far, ((k, k_t),))
 
     for c in range(2):
         @pl.when(chip == c)

time: 89 us -> 89.1 us (level)
  no operation moved by 1% of the time
where the time goes in v8:
time: 89.1 us; the launch traced here: 89 us
  Pallas kernels  88.1 us (99%)
    pallas_call x1, Pallas kernels, fused_step(): pl.pallas_call(body, out_shape=(pltpu.VMEM((BLK, DIM), BF16), pltpu.VMEM(...  85.6 us
    pallas_call x1, Pallas kernels, flush(): pl.pallas_call(flush_body, out_shape=tuple((jax.ShapeDtypeStruct(a.shape,...  2.57 us

profile of v8, /device:TPU:0, one launch (start us, length us, event | category | flops | bytes accessed | tf_op | source)
XLA Modules:
  0.0 89.0 jit_solution(1727795346500243594)
XLA Ops:
  0.6 85.6 %attention_backward.1 = (bf16[256,2048]{1,0:T(8,128)(2,1)S(1)}, f32[1024,2,256]{2,1,0:T(2,128)S(1)}, f32[256,256]{1,0:T(8,128)S(1)}, f32[256,256]{1,0:T(8,128)S(1)}, f32[512,1024]{1,0:T(8,128)S(1)}) custom-call(bf16[256,2048]{1,0:T(8,128)(2,1)} %bitcast.8, bf16[256,2048]{1,0:T(8,128)(2,1)} %bitcast.9, bf16[2048,2,256]{2,1,0:T(2,128)(2,1)} %wq_ref.1, ...), custom_call_target="tpu_custom_call" | custom-call | tf_op jit(solution)/shard_map/attention_backward/pallas_call | solution.py:553
  86.2 2.6 %write_results.1 = (bf16[256,2048]{1,0:T(8,128)(2,1)}, f32[1024,2,256]{2,1,0:T(2,128)}, f32[256,256]{1,0:T(8,128)}, f32[256,256]{1,0:T(8,128)}, f32[512,1024]{1,0:T(8,128)}) custom-call(bf16[256,2048]{1,0:T(8,128)(2,1)S(1)} %get-tuple-element.15.refs_0_, f32[1024,2,256]{2,1,0:T(2,128)S(1)} %get-tuple-element.16.refs_1_, ...), custom_call_target="tpu_custom_call" | custom-call | tf_op jit(solution)/shard_map/write_results/pallas_call | solution.py:580
